TPU v7x, 16 devices: a 4x2x1 block of a 4x4x8 slice. The times are simulated.
16 devices in a mesh: dp: 2 (over y, z), tp: 8 (over x, core).
Axes of the slice: x: 4, y: 2, z: 1, core: 2. Of those that a mesh axis runs over, the one named last changes fastest.
The devices are a block of a 4x4x8 slice.
Arguments:
- hidden: bfloat16 [4096, 512], P(('dp', 'tp')), parts along dimension 0
- ln_gain: float32 [512], replicated
- ln_bias: float32 [512], replicated
- out_embed: bfloat16 [32768, 512], P('tp')
- vocab_valid: int32 [32768], P('tp')
- targets: int32 [4096], P(('dp', 'tp')), parts along dimension 0
- loss_mask: int32 [4096], P(('dp', 'tp')), parts along dimension 0
Outputs:
- output 1: float32 [4096], P(('dp', 'tp')), parts along dimension 0
- output 2: float32 [2], P('dp'), parts along dimension 0
- output 3: bfloat16 [4096, 512], P(('dp', 'tp')), parts along dimension 0
- output 4: float32 [65536, 512], P(('dp', 'tp')), parts along dimension 0
- output 5: float32 [1024], P('dp'), parts along dimension 0
- output 6: float32 [1024], P('dp'), parts along dimension 0
There are 2 independent parts. A program takes and returns all parts, laid end to end along the dimension named above; an argument that names none is the same for every part.
All inputs are finite; a program needn't handle non-finite values.
Results may differ from a plain program's by a relative error of at most 0.001.
Values are sent between devices in bfloat16 or wider.
A program may use at most 768 MiB of HBM per device.

v0:
```python
import jax
import jax.numpy as jnp
from jax import lax
from jax.sharding import PartitionSpec as P

SOFT_CAP = 30.0
Z_COEF = 1e-4
LN_EPS = 1e-5


def layer_norm(h_float, ln_gain, ln_bias):
    mean_val = jnp.mean(h_float, axis=-1, keepdims=True)
    centered = h_float - mean_val
    var_val = jnp.mean(centered * centered, axis=-1, keepdims=True)
    return centered * lax.rsqrt(var_val + LN_EPS) * ln_gain + ln_bias


def solution(mesh):
    def group_step(hidden, ln_gain, ln_bias, out_embed, vocab_valid, targets, loss_mask):
        rows_loc = hidden.shape[0]
        vocab_loc = out_embed.shape[0]
        shard_idx = lax.axis_index("tp")
        normed, ln_back = jax.vjp(layer_norm, hidden.astype(jnp.float32), ln_gain, ln_bias)
        x_all = lax.all_gather(normed.astype(jnp.bfloat16), "tp", axis=0, tiled=True)
        tgt_all = lax.all_gather(targets, "tp", axis=0, tiled=True)
        mask_all = lax.all_gather(loss_mask, "tp", axis=0, tiled=True).astype(jnp.float32)
        logits = lax.dot_general(x_all, out_embed, (((1,), (1,)), ((), ())), preferred_element_type=jnp.float32)
        tanh_val = jnp.tanh(logits / SOFT_CAP)
        capped = SOFT_CAP * tanh_val
        col_ok = (vocab_valid != 0)[None, :]
        masked = jnp.where(col_ok, capped, -SOFT_CAP)
        glob_max = lax.pmax(jnp.max(masked, axis=1), "tp")
        exp_vals = jnp.where(col_ok, jnp.exp(masked - glob_max[:, None]), 0.0)
        col_ids = shard_idx * vocab_loc + jnp.arange(vocab_loc)
        is_target = tgt_all[:, None] == col_ids[None, :]
        local_stats = jnp.stack([jnp.sum(exp_vals, axis=1), jnp.sum(jnp.where(is_target, capped, 0.0), axis=1)])
        group_stats = lax.psum(local_stats, "tp")
        sum_exp = group_stats[0]
        lse = glob_max + jnp.log(sum_exp)
        tok_count = jnp.sum(mask_all)
        loss_all = (lse - group_stats[1] + Z_COEF * lse * lse) * mask_all
        mean_loss = jnp.sum(loss_all) / tok_count
        tok_coef = mask_all / tok_count
        prob_coef = (1.0 + 2.0 * Z_COEF * lse) * tok_coef / sum_exp
        d_capped = prob_coef[:, None] * exp_vals - jnp.where(is_target, tok_coef[:, None], 0.0)
        d_logits = (d_capped * (1.0 - tanh_val * tanh_val)).astype(jnp.bfloat16)
        d_embed = lax.dot_general(d_logits, x_all, (((0,), (0,)), ((), ())), preferred_element_type=jnp.float32)
        dx_part = jnp.dot(d_logits, out_embed, preferred_element_type=jnp.float32)
        d_normed = lax.psum_scatter(dx_part, "tp", scatter_dimension=0, tiled=True)
        d_hidden, gain_part, bias_part = ln_back(d_normed)
        d_gain = lax.psum(gain_part, "tp")
        d_bias = lax.psum(bias_part, "tp")
        tok_loss = lax.dynamic_slice_in_dim(loss_all, shard_idx * rows_loc, rows_loc)
        return tok_loss, mean_loss.reshape(1), d_hidden.astype(jnp.bfloat16), d_embed, d_gain, d_bias

    row_spec = P(("dp", "tp"))
    mat_spec = P(("dp", "tp"), None)
    return jax.shard_map(group_step, mesh=mesh, in_specs=(mat_spec, P(None), P(None), P("tp", None), P("tp"), row_spec, row_spec), out_specs=(row_spec, P("dp"), mat_spec, mat_spec, P("dp"), P("dp")), check_vma=False)
```

profile of v0, /device:TPU:113, one launch (start us, length us, event | category | flops | bytes accessed | tf_op | source)
XLA Modules:
  0.0 232.5 jit_solution(2501318183179020798)
XLA Ops:
  7.2 0.1 all-gather.4.cloned.1.call-start
  7.2 1.1 convert_reduce_fusion
  8.3 1.2 fusion.15
  9.5 1.9 fusion.13
  11.4 0.1 all-gather.4.cloned.1.call-update
  11.4 0.1 reduce-scatter.2.cloned.1.call-start
  11.5 20.1 %all-gather.1 = s32[8,1,256]{2,1,0:T(1,128)S(1)} all-gather(s32[1,1,256]{2,1,0:T(1,128)} %bitcast.22), channel_id=1, replica_groups=mesh['dp'=2,'tp'=8] {'tp'}, dimensions={0}, use_global_device_ids=true | all-gather | bytes 9216 | tf_op jit(solution)/shard_map/all_gather | solution.py:26
  31.6 20.1 %all-gather = s32[8,1,256]{2,1,0:T(1,128)S(1)} all-gather(s32[1,1,256]{2,1,0:T(1,128)} %bitcast.23), channel_id=1, replica_groups=mesh['dp'=2,'tp'=8] {'tp'}, dimensions={0}, use_global_device_ids=true | all-gather | bytes 9216 | tf_op jit(solution)/shard_map/all_gather | solution.py:25
  51.7 0.6 convert_reduce_fusion.1
  52.3 0.7 broadcast_compare_fusion
  53.0 0.0 all-gather.4.cloned.1.call-done
  53.0 18.8 %select_reduce_fusion = (f32[2048]{0:T(1024)S(1)}, f32[2048,4096]{1,0:T(8,128)}) fusion(pred[4096]{0:T(1024)(128)(4,1)S(1)} %broadcast_compare_fusion, bf16[2048,512]{1,0:T(8,128)(2,1)} %all-gather.4.cloned.1.call-done, bf16[4096,512]{1,0:T(8,128)(2,1)} %param.10), kind=kOutput, calls=%fused_computation.8 | convolution fusion | flops 8623486976 | bytes 39858176 | tf_op jit(solution)/shard_map/dot_general | solution.py:27
  71.9 18.0 %pmax.7 = f32[2048]{0:T(1024)S(1)} all-reduce(f32[2048]{0:T(1024)S(1)} %get-tuple-element.23), channel_id=1, replica_groups=mesh['dp'=2,'tp'=8] {'tp'}, use_global_device_ids=true, to_apply=%region_3.4 | all-reduce | flops 2048 | bytes 16384 | tf_op jit(solution)/shard_map/pmax | solution.py:32
  89.8 21.4 %fusion.5 = (f32[2048]{0:T(1024)S(1)}, f32[2048]{0:T(1024)S(1)}) fusion(f32[2048,4096]{1,0:T(8,128)} %get-tuple-element.24, f32[2048]{0:T(1024)S(1)} %pmax.7, pred[4096]{0:T(1024)(128)(4,1)S(1)} %broadcast_compare_fusion, s32[4096]{0:T(1024)S(1)} %iota_add_fusion, s32[2048]{0:T(1024)S(1)} %bitcast.15), kind=kLoop, calls=%fused_computation.10 | loop fusion | flops 75493376 | bytes 33607680 | tf_op jit(solution)/shard_map/reduce_sum | solution.py:36
  111.3 21.0 %psum.21 = f32[2,2048]{1,0:T(2,128)S(1)} all-reduce(f32[2,2048]{1,0:T(2,128)S(1)} %pad_maximum_fusion), channel_id=1, replica_groups=mesh['dp'=2,'tp'=8] {'tp'}, use_global_device_ids=true, to_apply=%region_6.7 | all-reduce | flops 4096 | bytes 32768 | tf_op jit(solution)/shard_map/psum | solution.py:37
  132.2 0.0 copy-start.3
  132.3 1.4 multiply_divide_fusion
  133.7 21.9 %fusion.3 = bf16[2048,4096]{1,0:T(8,128)(2,1)S(1)} fusion(f32[2048,4096]{1,0:T(8,128)} %get-tuple-element.24, f32[2048]{0:T(1024)S(1)} %get-tuple-element.16, f32[2048]{0:T(1024)S(1)} %get-tuple-element.15, s32[4096]{0:T(1024)S(1)} %iota_add_fusion, f32[2048]{0:T(1024)S(1)} %pmax.7, s32[2048]{0:T(1024)S(1)} %bitcast.16, ...), kind=kLoop, calls=%fused_computation.5 | loop fusion | flops 109051904 | bytes 50384896 | tf_op jit(solution)/shard_map/convert_element_type | solution.py:46
  155.6 0.0 copy-start
  155.6 5.7 %copy-done = bf16[2048,4096]{1,0:T(8,128)(2,1)} copy-done((bf16[2048,4096]{1,0:T(8,128)(2,1)}, bf16[2048,4096]{1,0:T(8,128)(2,1)S(1)}, u32[]{:S(2)}) %copy-start) | copy-done | bytes 16777240
  161.3 0.0 copy-done.3
  161.3 0.0 copy-start.4
  161.3 10.3 %fusion.24 = f32[2048,512]{1,0:T(8,128)} fusion(bf16[2048,4096]{1,0:T(8,128)(2,1)S(1)} %fusion.3, bf16[4096,512]{1,0:T(8,128)(2,1)S(1)} %copy-done.3), kind=kOutput, calls=%fused_computation.44 | convolution fusion | flops 8589934592 | bytes 25165824 | tf_op jit(solution)/shard_map/dot_general | solution.py:48
  171.6 0.1 reduce-scatter.2.cloned.1.call-update
  171.7 0.0 copy-start.1
  171.7 0.0 copy-start.2
  173.1 0.6 dynamic_slice.3
  173.7 0.0 copy-done.4
  173.7 14.5 %fusion.25 = f32[4096,512]{1,0:T(8,128)} fusion(bf16[2048,4096]{1,0:T(8,128)(2,1)} %copy-done, bf16[2048,512]{1,0:T(8,128)(2,1)S(1)} %copy-done.4), kind=kOutput, calls=%fused_computation.45 | convolution fusion | flops 8589934592 | bytes 27262976 | tf_op jit(solution)/shard_map/dot_general | solution.py:47
  188.2 16.9 %reduce-scatter.2.cloned.1.call-done = f32[256,512]{1,0:T(8,128)} async-done(((f32[2048,512]{1,0:T(8,128)}), f32[256,512]{1,0:T(8,128)}) %reduce-scatter.2.cloned.1.call-update) | async-done | bytes 524304 | tf_op jit(solution)/shard_map/reduce_scatter | solution.py:49
  205.1 0.0 copy-done.1
  205.1 0.0 copy-done.2
  205.1 1.3 fusion.14
  206.5 1.3 fusion.20
  207.8 0.8 add_convert_fusion
  208.6 15.9 %all-reduce = (f32[512]{0:T(512)}, f32[512]{0:T(512)}) all-reduce(f32[512]{0:T(512)S(1)} %get-tuple-element.8, f32[512]{0:T(512)S(1)} %get-tuple-element.10), channel_id=1, replica_groups=mesh['dp'=2,'tp'=8] {'tp'}, use_global_device_ids=true, to_apply=%region_13.14 | all-reduce | flops 1024 | bytes 8192 | tf_op jit(solution)/shard_map/psum | solution.py:51
  (8 shorter events, 0.1 us)
Async XLA Ops:
  7.2 45.9 %all-gather.4.cloned.1.call-start = ((), (), s32[]{:S(2)}) async-start(), calls=%async_computation.1 | async-start | bytes 2359296 | tf_op jit(solution)/shard_map/all_gather | solution.py:24
  11.4 193.7 %reduce-scatter.2.cloned.1.call-start = ((), (), s32[]{:S(2)}) async-start(), calls=%async_computation.2 | async-start | bytes 4718592 | tf_op jit(solution)/shard_map/reduce_scatter | solution.py:49
  132.2 29.1 %copy-start.3 = (bf16[4096,512]{1,0:T(8,128)(2,1)S(1)}, bf16[4096,512]{1,0:T(8,128)(2,1)}, u32[]{:S(2)}) copy-start(bf16[4096,512]{1,0:T(8,128)(2,1)} %param.10) | copy-start | bytes 12582916
  155.6 5.7 %copy-start = (bf16[2048,4096]{1,0:T(8,128)(2,1)}, bf16[2048,4096]{1,0:T(8,128)(2,1)S(1)}, u32[]{:S(2)}) copy-start(bf16[2048,4096]{1,0:T(8,128)(2,1)S(1)} %fusion.3) | copy-start | bytes 50331652
  161.3 12.4 %copy-start.4 = (bf16[2048,512]{1,0:T(8,128)(2,1)S(1)}, bf16[2048,512]{1,0:T(8,128)(2,1)}, u32[]{:S(2)}) copy-start(bf16[2048,512]{1,0:T(8,128)(2,1)} %all-gather.4.cloned.1.call-done) | copy-start | bytes 6291460
  171.7 33.5 %copy-start.1 = (bf16[256,512]{1,0:T(8,128)(2,1)S(1)}, bf16[256,512]{1,0:T(8,128)(2,1)}, u32[]{:S(2)}) copy-start(bf16[256,512]{1,0:T(8,128)(2,1)} %param.7) | copy-start | bytes 786436
  171.7 33.4 %copy-start.2 = (f32[512]{0:T(512)S(1)}, f32[512]{0:T(512)}, u32[]{:S(2)}) copy-start(f32[512]{0:T(512)} %param.8) | copy-start | bytes 6148
Sparse Core Ops, SparseCore 0:
  11.5 24.3 all-gather.3
  171.8 33.2 reduce-scatter.1
where the time goes:
time: 233 us
  blocking collectives  95.1 us (41%)
  other arithmetic  53.7 us (23%)
  matrix products  43.6 us (19%)
  waiting for transfers between devices  17 us (7%)
  between operations  16.7 us (7%)
  local copies, waits for them, and re-layouts  6.38 us (3%)
    convert_element_type x1, other arithmetic, group_step(): d_logits = (d_capped * (1.0 - tanh_val * tanh_val)).astype(jnp.bfloat16)  21.9 us
    reduce_sum x1, other arithmetic, group_step(): jnp.sum(exp_vals, axis=1)  21.4 us
    psum x1, blocking collectives, group_step(): group_stats = lax.psum(local_stats, 'tp')  21 us
    all_gather x1, blocking collectives, group_step(): tgt_all = lax.all_gather(targets, 'tp', axis=0, tiled=True)  20.1 us
    all_gather x1, blocking collectives, group_step(): lax.all_gather(loss_mask, 'tp', axis=0, tiled=True).astype(jnp.float32)  20.1 us
    dot_general x1, matrix products, group_step(): lax.dot_general(x_all, out_embed, (((1,), (1,)), ((), ())), preferred_ele...  18.8 us
    pmax x1, blocking collectives, group_step(): glob_max = lax.pmax(jnp.max(masked, axis=1), 'tp')  18 us
    reduce_scatter x1, waiting for transfers between devices, group_step(): d_normed = lax.psum_scatter(dx_part, 'tp', scatter_dimension=0, tiled=True)  16.9 us
  transfers between devices with their start and end apart: 2, of which 1 were waited for; matrix products, arithmetic and copies ran while one was open for 7% of the time, Pallas kernels for 0%

commit v1 on v0

v1 whole, which is shorter than its diff:
```python
import functools

import jax
import jax.numpy as jnp
from jax import lax
from jax.experimental import pallas as pl
from jax.experimental.pallas import tpu as pltpu
from jax.sharding import PartitionSpec as P

SOFT_CAP = 30.0
Z_COEF = 1e-4
LN_EPS = 1e-5
EXP_SCALE = SOFT_CAP * 1.4426950408889634
MESH = pl.DeviceIdType.MESH
CHIPS = 4
OFFSET = (0, 1, 3, 2)
OWN, RIGHT, LEFT, OPP = range(4)
HT = 128
SUB = 32

TO_PARTNER, TO_RIGHT, TO_LEFT, FWD_RIGHT, FWD_LEFT, REL_LEFT, REL_RIGHT, REL_OPP_A, REL_OPP_B = range(9)
PAIR, OPP_RIGHT, OPP_LEFT, RIGHT_HI, RIGHT_LO, LEFT_LO, LEFT_HI = 0, 4, 5, 6, 7, 8, 9


def norm(h):
    mean = jnp.mean(h, axis=-1, keepdims=True)
    cent = h - mean
    rstd = lax.rsqrt(jnp.mean(cent * cent, axis=-1, keepdims=True) + LN_EPS)
    return cent * rstd, rstd


def kernel(
    hid, gain, bias, e_hbm, valid, tgt, msk,
    loss_out, mean_out, dh_out, de_hbm, gb_out,
    x_all, xt, e, et, vb, w, dz, tm_all, st_send, st_recv, av, dv, ls, dx, d2d, ring, fin, gb_send, gb_recv, stage,
    e_sem, out_sem, tm_s, tm_r, ag_s, ag_r, st_s, st_r, rs_s, rs_r, gb_s, gb_r,
    *, vc, ec,
):
    group = 2 * CHIPS
    me = lax.axis_index("tp")
    c, k = me // 2, me % 2
    other = 1 - k
    partner = 2 * c + other
    chip = [(c + o) % CHIPS for o in OFFSET]
    right, left = 2 * chip[RIGHT] + k, 2 * chip[LEFT] + k
    vocab, dim = e_hbm.shape
    nv, ne = vocab // vc, vocab // ec

    def remote(src, dst, send, recv, dev):
        return pltpu.make_async_remote_copy(
            src_ref=src, dst_ref=dst, send_sem=send, recv_sem=recv, device_id={"tp": dev}, device_id_type=MESH
        )

    e_copies = [
        pltpu.make_async_copy(e_hbm.at[pl.ds(i * vc, vc)], e.at[pl.ds(i * vc, vc)], e_sem.at[i]) for i in range(nv)
    ]
    for cp in e_copies:
        cp.start()

    barrier = pltpu.get_barrier_semaphore()
    for j in range(1, group):
        pl.semaphore_signal(barrier, inc=1, device_id={"tp": (me + j) % group}, device_id_type=MESH)

    for h in range(2):
        xh, _ = norm(hid[h * HT : (h + 1) * HT, :].astype(jnp.float32))
        x_all[h, c, k] = (xh * gain[...] + bias[...]).astype(jnp.bfloat16)
    tm_all[me] = tgt[...] * 2 + msk[...]

    pl.semaphore_wait(barrier, group - 1)

    def ag(h, i, src, dst, dev):
        return remote(src, dst, ag_s.at[h * 9 + i], ag_r.at[h * 9 + i], dev)

    def lo(ref):
        return ref.at[pl.ds(0, HT // 2)]

    def hi(ref):
        return ref.at[pl.ds(HT // 2, HT // 2)]

    def block(h, r, core):
        return x_all.at[h, chip[r], core]

    def ag_copy(h, i):
        mine, lft, rgt, opp = block(h, OWN, k), block(h, LEFT, k), block(h, RIGHT, k), block(h, OPP, k)
        src, dev = {
            TO_PARTNER: (mine, partner),
            TO_RIGHT: (mine, right),
            TO_LEFT: (mine, left),
            FWD_RIGHT: (lo(lft), right),
            FWD_LEFT: (hi(rgt), left),
            REL_LEFT: (lft, partner),
            REL_RIGHT: (rgt, partner),
            REL_OPP_A: (lo(opp), partner),
            REL_OPP_B: (hi(opp), partner),
        }[i]
        return ag(h, i, src, src, dev)

    def ag_arrival(h, i):
        ref = {
            TO_PARTNER: block(h, OWN, other),
            TO_RIGHT: block(h, LEFT, k),
            TO_LEFT: block(h, RIGHT, k),
            FWD_RIGHT: lo(block(h, OPP, k)),
            FWD_LEFT: hi(block(h, OPP, k)),
            REL_LEFT: block(h, LEFT, other),
            REL_RIGHT: block(h, RIGHT, other),
            REL_OPP_A: lo(block(h, OPP, other)),
            REL_OPP_B: hi(block(h, OPP, other)),
        }[i]
        ag(h, i, ref, ref, partner).wait_recv()

    started = []

    def go(copy):
        copy.start()
        started.append(copy)

    def tm_copy(j):
        return remote(tm_all.at[me], tm_all.at[me], tm_s.at[j - 1], tm_r.at[j - 1], (me + j) % group)

    for h in range(2):
        if h == 0:
            for j in range(1, group):
                go(tm_copy(j))
        for i in (TO_PARTNER, TO_RIGHT, TO_LEFT):
            go(ag_copy(h, i))

    def tm_arrival(j):
        ref = tm_all.at[(me - j + group) % group]
        remote(ref, ref, tm_s.at[j - 1], tm_r.at[j - 1], partner).wait_recv()

    @pl.loop(0, vocab // 128)
    def _(i):
        row = jnp.broadcast_to(valid[pl.ds(i, 1), :].astype(jnp.float32), (128, 128))
        vb[pl.ds(pl.multiple_of(i * 128, 128), 128), :] = row.T

    for cp in e_copies:
        cp.wait()

    iota = lax.broadcasted_iota(jnp.int32, (SUB, 256), 0).reshape(SUB // 8, 8, 256)

    def local_target(h, chip_no):
        halves = [
            jnp.broadcast_to((tm_all[2 * chip_no + kk, pl.ds(h, 1), :] >> 1) - me * vocab, (8, 128)) for kk in range(2)
        ]
        return jnp.concatenate(halves, axis=1)

    def forward(h, r, slot):
        chip_no = chip[r]
        xt[...] = x_all[h, chip_no].reshape(2 * HT, dim).T
        tgt8 = local_target(h, chip_no)

        def body(i, carry):
            s_acc, t_acc = carry
            rows0 = pl.multiple_of(i * vc, vc)
            z = jnp.dot(e[pl.ds(rows0, vc), :], xt[...], preferred_element_type=jnp.float32)
            tgt_rel = tgt8 - rows0
            for j in range(vc // SUB):
                rows = pl.ds(pl.multiple_of(rows0 + j * SUB, SUB), SUB)
                ok = vb[rows, :]
                ok = jnp.concatenate([ok, ok], axis=1)
                t = jnp.tanh(z[j * SUB : (j + 1) * SUB, :] * (1.0 / SOFT_CAP))
                ex = jnp.exp2(t * EXP_SCALE) * ok
                w[slot, rows, :] = ex * (1.0 - t * t)
                hit = iota == (tgt_rel - j * SUB)[None]
                s_acc = s_acc + jnp.sum(ex.reshape(SUB // 8, 8, 256), axis=0)
                t_acc = t_acc + jnp.sum(jnp.where(hit, t.reshape(SUB // 8, 8, 256), 0.0), axis=0)
            return s_acc, t_acc

        zero = jnp.zeros((8, 256), jnp.float32)
        s_acc, t_acc = lax.fori_loop(0, nv, body, (zero, zero))
        s_row = jnp.sum(s_acc, axis=0, keepdims=True)
        t_row = jnp.sum(t_acc, axis=0, keepdims=True)
        for kk in range(2):
            st_send[h, pl.ds(2 * chip_no + kk, 1), :] = s_row[:, kk * 128 : (kk + 1) * 128]
            st_send[h, pl.ds(group + 2 * chip_no + kk, 1), :] = t_row[:, kk * 128 : (kk + 1) * 128]

    def st_copy(h, j):
        n = h * (group - 1) + j - 1
        return remote(st_send.at[h], st_recv.at[h, j - 1], st_s.at[n], st_r.at[n], (me + j) % group)

    def stats_start(h):
        for j in range(1, group):
            go(st_copy(h, j))

    def token_count():
        total = jnp.zeros((2, 128), jnp.int32)
        for p in range(group):
            total = total + (tm_all[p] & 1)
        total = jnp.sum(jnp.sum(total.astype(jnp.float32), axis=1, keepdims=True), axis=0, keepdims=True)
        return total

    def stats_finish(h):
        tot = st_send[h]
        for j in range(1, group):
            st_copy(h, j).wait_recv()
        for j in range(1, group):
            tot = tot + st_recv[h, j - 1]
        s, t = tot[:group], tot[group:]
        mask = jnp.concatenate([tm_all[p, pl.ds(h, 1), :] & 1 for p in range(group)], axis=0).astype(jnp.float32)
        lse = jnp.log(s)
        coef = mask / token_count()
        a = (1.0 + 2.0 * Z_COEF * lse) * coef / s
        av[h] = a
        dv[h] = (a * jnp.exp2(t * EXP_SCALE) - coef) * (1.0 - t * t)
        ls[h] = (lse - SOFT_CAP * t + Z_COEF * lse * lse) * mask

    def spread(ref, h, chip_no):
        return jnp.concatenate(
            [jnp.broadcast_to(ref[h, pl.ds(2 * chip_no + kk, 1), :], (8, 128)) for kk in range(2)], axis=1
        )

    def backward(h, r, slot):
        chip_no = chip[r]
        tile = h * CHIPS + chip_no
        tgt8 = local_target(h, chip_no)
        a8, d8 = spread(av, h, chip_no)[None], spread(dv, h, chip_no)[None]
        for kk in range(2):
            dx[h, r, kk] = jnp.zeros((dim, HT), jnp.float32)

        @pl.loop(0, nv)
        def _(i):
            rows0 = pl.multiple_of(i * vc, vc)
            tgt_rel = tgt8 - rows0
            pieces = []
            for j in range(vc // SUB):
                rows = pl.ds(pl.multiple_of(rows0 + j * SUB, SUB), SUB)
                hit = iota == (tgt_rel - j * SUB)[None]
                g = jnp.where(hit, d8, a8 * w[slot, rows, :].reshape(SUB // 8, 8, 256))
                g = g.reshape(SUB, 256).astype(jnp.bfloat16)
                dz[tile, rows, :] = g
                pieces.append(g)
            part = jnp.dot(et[i], jnp.concatenate(pieces, axis=0), preferred_element_type=jnp.float32)
            for kk in range(2):
                dx[h, r, kk] += part[:, kk * HT : (kk + 1) * HT]

    dlo, dhi = pl.ds(0, dim // 2), pl.ds(dim // 2, dim // 2)

    def rs(h, i, src, dst, dev):
        return remote(src, dst, rs_s.at[h * 10 + i], rs_r.at[h * 10 + i], dev)

    def pair_start(h, r):
        go(rs(h, PAIR + r, dx.at[h, r, other], d2d.at[h, r], partner))

    def pair_finish(h, r):
        rs(h, PAIR + r, d2d.at[h, r], d2d.at[h, r], partner).wait_recv()
        dx[h, r, k] = dx[h, r, k] + d2d[h, r]

    def opp_send(h):
        pair_finish(h, OPP)
        go(rs(h, OPP_RIGHT, dx.at[h, OPP, k, dlo], ring.at[h, 0], right))
        go(rs(h, OPP_LEFT, dx.at[h, OPP, k, dhi], ring.at[h, 1], left))

    def right_send(h):
        pair_finish(h, RIGHT)
        go(rs(h, RIGHT_HI, dx.at[h, RIGHT, k, dhi], fin.at[h, 0, dhi], right))

    def left_send(h):
        pair_finish(h, LEFT)
        go(rs(h, LEFT_LO, dx.at[h, LEFT, k, dlo], fin.at[h, 1, dlo], left))

    def ring_send(h):
        rs(h, OPP_RIGHT, ring.at[h, 0], ring.at[h, 0], partner).wait_recv()
        dx[h, RIGHT, k, dlo] = dx[h, RIGHT, k, dlo] + ring[h, 0]
        go(rs(h, RIGHT_LO, dx.at[h, RIGHT, k, dlo], fin.at[h, 0, dlo], right))
        rs(h, OPP_LEFT, ring.at[h, 1], ring.at[h, 1], partner).wait_recv()
        dx[h, LEFT, k, dhi] = dx[h, LEFT, k, dhi] + ring[h, 1]
        go(rs(h, LEFT_HI, dx.at[h, LEFT, k, dhi], fin.at[h, 1, dhi], left))

    def finish(h):
        for i, n, part in ((RIGHT_HI, 0, dhi), (RIGHT_LO, 0, dlo), (LEFT_LO, 1, dlo), (LEFT_HI, 1, dhi)):
            rs(h, i, fin.at[h, n, part], fin.at[h, n, part], partner).wait_recv()
        dn = (dx[h, OWN, k] + fin[h, 0] + fin[h, 1]).T
        xh, rstd = norm(hid[h * HT : (h + 1) * HT, :].astype(jnp.float32))
        dxh = dn * gain[...]
        m1 = jnp.mean(dxh, axis=-1, keepdims=True)
        m2 = jnp.mean(dxh * xh, axis=-1, keepdims=True)
        dh_out[h * HT : (h + 1) * HT, :] = (rstd * (dxh - m1 - xh * m2)).astype(jnp.bfloat16)
        return jnp.sum(dn * xh, axis=0, keepdims=True), jnp.sum(dn, axis=0, keepdims=True)

    def out_copy(i, slot):
        return pltpu.make_async_copy(
            stage.at[slot], de_hbm.at[pl.ds(pl.multiple_of(i * ec, ec), ec)], out_sem.at[slot]
        )

    def embed(first, last):
        @pl.loop(first, last)
        def _(i):
            slot = i % 2

            @pl.when(i >= 2)
            def _():
                out_copy(i - 2, slot).wait()

            rows = pl.ds(pl.multiple_of(i * ec, ec), ec)
            acc = None
            for tile in range(2 * CHIPS):
                xx = x_all[tile // CHIPS, tile % CHIPS].reshape(2 * HT, dim)
                part = jnp.dot(dz[tile, rows, :], xx, preferred_element_type=jnp.float32)
                acc = part if acc is None else acc + part
            stage[slot] = acc
            out_copy(i, slot).start()

    jp = 6 - 6 * k
    ref0 = tm_all.at[0]
    remote(ref0, ref0, tm_s.at[jp], tm_r.at[jp], partner).wait_recv()
    ag_arrival(0, TO_PARTNER)
    forward(0, OWN, 0)
    ag_arrival(1, TO_PARTNER)
    forward(1, OWN, 1)
    for i in range(1, group - 1):
        n = (jp + i) % (group - 1)
        remote(ref0, ref0, tm_s.at[n], tm_r.at[n], partner).wait_recv()

    def ag_pass(h):
        ag_arrival(h, TO_RIGHT)
        ag_arrival(h, TO_LEFT)
        for i in (FWD_RIGHT, FWD_LEFT, REL_RIGHT, REL_LEFT):
            go(ag_copy(h, i))

    def ag_pass_opp(h):
        ag_arrival(h, FWD_RIGHT)
        ag_arrival(h, FWD_LEFT)
        for i in (REL_OPP_A, REL_OPP_B):
            go(ag_copy(h, i))

    ag_pass(0)
    ag_arrival(0, REL_RIGHT)
    forward(0, RIGHT, 2)
    ag_pass(1)
    ag_arrival(0, REL_LEFT)
    forward(0, LEFT, 3)
    ag_pass_opp(0)
    ag_arrival(0, REL_OPP_A)
    ag_arrival(0, REL_OPP_B)
    forward(0, OPP, 4)
    stats_start(0)

    @pl.loop(0, nv)
    def _(i):
        et[i] = e[pl.ds(pl.multiple_of(i * vc, vc), vc), :].T

    ag_pass_opp(1)
    stats_finish(0)
    backward(0, OPP, 4)
    pair_start(0, OPP)
    ag_arrival(1, REL_RIGHT)
    forward(1, RIGHT, 4)
    opp_send(0)
    backward(0, RIGHT, 2)
    pair_start(0, RIGHT)
    ag_arrival(1, REL_LEFT)
    forward(1, LEFT, 2)
    right_send(0)
    backward(0, LEFT, 3)
    pair_start(0, LEFT)
    ag_arrival(1, REL_OPP_A)
    ag_arrival(1, REL_OPP_B)
    forward(1, OPP, 3)
    stats_start(1)
    left_send(0)
    ring_send(0)
    backward(0, OWN, 0)
    pair_start(0, OWN)
    stats_finish(1)
    loss_out[...] = jnp.concatenate([ls[h, pl.ds(me, 1), :] for h in range(2)], axis=0)
    both = ls[0] + ls[1]
    mean_out[...] = jnp.sum(jnp.sum(both, axis=1, keepdims=True), axis=0, keepdims=True) / token_count()
    backward(1, OPP, 3)
    pair_start(1, OPP)
    pair_finish(0, OWN)
    backward(1, RIGHT, 4)
    pair_start(1, RIGHT)
    opp_send(1)
    backward(1, LEFT, 2)
    pair_start(1, LEFT)
    right_send(1)
    backward(1, OWN, 1)
    pair_start(1, OWN)
    left_send(1)
    quarter = ne // 4
    embed(0, quarter)
    pair_finish(1, OWN)
    embed(quarter, 2 * quarter)
    ring_send(1)
    embed(2 * quarter, 3 * quarter)
    g0, b0 = finish(0)
    embed(3 * quarter, ne)
    g1, b1 = finish(1)
    g, b = g0 + g1, b0 + b1
    for i in range(4):
        gb_send[i : i + 1, :] = g[:, i * 128 : (i + 1) * 128]
        gb_send[4 + i : 5 + i, :] = b[:, i * 128 : (i + 1) * 128]

    def gb_copy(j):
        return remote(gb_send, gb_recv.at[j - 1], gb_s.at[j - 1], gb_r.at[j - 1], (me + j) % group)

    for j in range(1, group):
        go(gb_copy(j))
    for i in range(ne - 2, ne):
        out_copy(i, i % 2).wait()
    tot = gb_send[...]
    for j in range(1, group):
        gb_copy(j).wait_recv()
        tot = tot + gb_recv[j - 1]
    gb_out[...] = tot
    for copy in started:
        copy.wait_send()


def solution(mesh):
    assert mesh.shape["tp"] == 2 * CHIPS

    def group_step(hidden, ln_gain, ln_bias, out_embed, vocab_valid, targets, loss_mask):
        rows, dim = hidden.shape
        vocab = out_embed.shape[0]
        group = 2 * CHIPS
        assert rows == 2 * HT
        vc, ec = 1024, 512
        nv = vocab // vc
        f32, bf16, i32 = jnp.float32, jnp.bfloat16, jnp.int32
        vmem = pl.BlockSpec(memory_space=pltpu.VMEM)
        hbm = pl.BlockSpec(memory_space=pl.ANY)
        dma = pltpu.SemaphoreType.DMA
        loss, mean, dh, de, gb = pl.pallas_call(
            functools.partial(kernel, vc=vc, ec=ec),
            out_shape=(
                jax.ShapeDtypeStruct((2, 128), f32),
                jax.ShapeDtypeStruct((1, 1), f32),
                jax.ShapeDtypeStruct((rows, dim), bf16),
                jax.ShapeDtypeStruct((vocab, dim), f32),
                jax.ShapeDtypeStruct((8, 128), f32),
            ),
            in_specs=[vmem, vmem, vmem, hbm, vmem, vmem, vmem],
            out_specs=(vmem, vmem, vmem, hbm, vmem),
            scratch_shapes=[
                pltpu.VMEM((2, CHIPS, 2, HT, dim), bf16),
                pltpu.VMEM((dim, 2 * HT), bf16),
                pltpu.VMEM((vocab, dim), bf16),
                pltpu.VMEM((nv, dim, vc), bf16),
                pltpu.VMEM((vocab, 128), f32),
                pltpu.VMEM((5, vocab, 2 * HT), f32),
                pltpu.VMEM((2 * CHIPS, vocab, 2 * HT), bf16),
                pltpu.VMEM((group, 2, 128), i32),
                pltpu.VMEM((2, 2 * group, 128), f32),
                pltpu.VMEM((2, group - 1, 2 * group, 128), f32),
                pltpu.VMEM((2, group, 128), f32),
                pltpu.VMEM((2, group, 128), f32),
                pltpu.VMEM((2, group, 128), f32),
                pltpu.VMEM((2, CHIPS, 2, dim, HT), f32),
                pltpu.VMEM((2, CHIPS, dim, HT), f32),
                pltpu.VMEM((2, 2, dim // 2, HT), f32),
                pltpu.VMEM((2, 2, dim, HT), f32),
                pltpu.VMEM((8, 128), f32),
                pltpu.VMEM((group - 1, 8, 128), f32),
                pltpu.VMEM((2, ec, dim), f32),
                dma((nv,)),
                dma((2,)),
                dma((group - 1,)),
                dma((group - 1,)),
                dma((18,)),
                dma((18,)),
                dma((2 * (group - 1),)),
                dma((2 * (group - 1),)),
                dma((20,)),
                dma((20,)),
                dma((group - 1,)),
                dma((group - 1,)),
            ],
            compiler_params=pltpu.CompilerParams(
                collective_id=0, has_side_effects=True, vmem_limit_bytes=67043328
            ),
            name="vocab_xent",
        )(
            hidden,
            ln_gain.reshape(1, dim),
            ln_bias.reshape(1, dim),
            out_embed,
            vocab_valid.reshape(vocab // 128, 128),
            targets.reshape(2, 128),
            loss_mask.reshape(2, 128),
        )
        return (
            loss.reshape(rows),
            mean.reshape(1),
            dh,
            de,
            gb[:4].reshape(dim),
            gb[4:].reshape(dim),
        )

    row_spec = P(("dp", "tp"))
    mat_spec = P(("dp", "tp"), None)
    return jax.shard_map(
        group_step,
        mesh=mesh,
        in_specs=(mat_spec, P(None), P(None), P("tp", None), P("tp"), row_spec, row_spec),
        out_specs=(row_spec, P("dp"), mat_spec, mat_spec, P("dp"), P("dp")),
        check_vma=False,
    )
```

time: 233 us -> 87.3 us (0.37)
  blocking collectives: 95.1 us -> 0 us
  Pallas kernels: 0 us -> 72.7 us
  other arithmetic: 53.7 us -> 0 us
  matrix products: 43.6 us -> 0 us
  waiting for transfers between devices: 17 us -> 0 us
  between operations: 16.7 us -> 2.41 us
  local copies, waits for them, and re-layouts: 6.38 us -> 11.9 us
    pallas_call x0 -> x1, Pallas kernels: none -> 72.7 us  [group_step(): pl.pallas_call(functools.partial(kernel, vc=vc, ec=ec), out_shape=(jax.Sh...]
    dot_general x3 -> x0, matrix products: 43.6 us -> none  [the longest x1 18.8 us: group_step(): lax.dot_general(x_all, out_embed, (((1,), (1,)), ((), ())), preferred_ele...]
    all_gather x2 -> x0, blocking collectives: 40.2 us -> none  [the longest x1 20.1 us: group_step(): tgt_all = lax.all_gather(targets, 'tp', axis=0, tiled=True)]
    psum x2 -> x0, blocking collectives: 36.9 us -> none  [the longest x1 21 us: group_step(): group_stats = lax.psum(local_stats, 'tp')]
    reduce_sum x6 -> x0, other arithmetic: 26.9 us -> none  [the longest x1 21.4 us: group_step(): jnp.sum(exp_vals, axis=1)]
    convert_element_type x4 -> x0, other arithmetic: 24.6 us -> none  [the longest x1 21.9 us: group_step(): d_logits = (d_capped * (1.0 - tanh_val * tanh_val)).astype(jnp.bfloat16)]
    pmax x1 -> x0, blocking collectives: 18 us -> none  [group_step(): glob_max = lax.pmax(jnp.max(masked, axis=1), 'tp')]
    reduce_scatter x1 -> x0, waiting for transfers between devices: 16.9 us -> none  [group_step(): d_normed = lax.psum_scatter(dx_part, 'tp', scatter_dimension=0, tiled=True)]
  transfers between devices with their start and end apart: 2 -> 0, of which waited for: 1 -> 0; matrix products, arithmetic and copies ran while one was open for 7% -> 0% of each run, Pallas kernels for 0% -> 0%
where the time goes in v1:
time: 87.3 us; the launch traced here: 87.1 us
  Pallas kernels  72.7 us (83%)
  local copies, waits for them, and re-layouts  11.9 us (14%)
  between operations  2.41 us (3%)
    pallas_call x1, Pallas kernels, group_step(): pl.pallas_call(functools.partial(kernel, vc=vc, ec=ec), out_shape=(jax.Sh...  72.7 us
    unnamed x3, local copies, waits for them, and re-layouts  10.6 us

profile of v1, /device:TPU:113, one launch (start us, length us, event | category | flops | bytes accessed | tf_op | source)
XLA Modules:
  0.0 87.1 jit_solution(4073378737080746306)
XLA Ops:
  0.6 72.7 %vocab_xent.1 = (f32[2,128]{1,0:T(2,128)}, f32[1,1]{1,0:T(1,128)}, bf16[256,512]{1,0:T(8,128)(2,1)}, f32[4096,512]{1,0:T(8,128)}, f32[8,128]{1,0:T(8,128)}) custom-call(bf16[256,512]{1,0:T(8,128)(2,1)} %hid.1, f32[1,512]{1,0:T(1,128)} %bitcast.12, f32[1,512]{1,0:T(1,128)} %bitcast.13, bf16[4096,512]{1,0:T(8,128)(2,1)} %e_hbm.1, s32[32,128]{1,0:T(8,128)} %bitcast.11, ...), custom_call_target="tpu_custom_call" | custom-call | tf_op jit(solution)/shard_map/vocab_xent/pallas_call | solution.py:425
  73.3 1.3 %slice_bitcast_fusion = (f32[512]{0:T(512)}, f32[512]{0:T(512)}) fusion(f32[8,128]{1,0:T(8,128)} %get-tuple-element.15), kind=kLoop, calls=%fused_computation | loop fusion | bytes 8192 | tf_op jit(solution)/shard_map/reshape | solution.py:489
  74.7 1.2 %copy.17 = f32[256]{0:T(256)} copy(f32[256]{0:T(256)} %bitcast.16) | data formatting | bytes 2048
  76.5 1.7 %copy.19 = bf16[256,512]{1,0:T(8,128)(2,1)} copy(bf16[256,512]{1,0:T(8,128)(2,1)} %get-tuple-element.26) | data formatting | bytes 524288
  78.2 7.8 %copy.20 = f32[4096,512]{1,0:T(8,128)} copy(f32[4096,512]{1,0:T(8,128)} %get-tuple-element.27) | data formatting | bytes 16777216

commit v2 on v1

--- a/solution.py
+++ b/solution.py
@@ -16,6 +16,9 @@
 OFFSET = (0, 1, 3, 2)
 OWN, RIGHT, LEFT, OPP = range(4)
 HT = 128
+CFG = (1024, 512, 1, 1, 6, 8)
+SLOTS = 6
+LIM = 54
 SUB = 32
 
 TO_PARTNER, TO_RIGHT, TO_LEFT, FWD_RIGHT, FWD_LEFT, REL_LEFT, REL_RIGHT, REL_OPP_A, REL_OPP_B = range(9)
@@ -31,10 +34,10 @@
 
 def kernel(
     hid, gain, bias, e_hbm, valid, tgt, msk,
-    loss_out, mean_out, dh_out, de_hbm, gb_out,
-    x_all, xt, e, et, vb, w, dz, tm_all, st_send, st_recv, av, dv, ls, dx, d2d, ring, fin, gb_send, gb_recv, stage,
-    e_sem, out_sem, tm_s, tm_r, ag_s, ag_r, st_s, st_r, rs_s, rs_r, gb_s, gb_r,
-    *, vc, ec,
+    de, loss_out, mean_out, dh_out, gain_out, bias_out,
+    dz, x_all, w, xt, e, et, vb, tm_all, st_send, st_recv, av, dv, ls, dx, d2d, ring, fin, gb_send, gb_recv, iota,
+    e_sem, tm_s, tm_r, ag_s, ag_r, st_s, st_r, rs_s, rs_r, gb_s, gb_r,
+    *, vc, ec, fu, bu, n1, n2,
 ):
     group = 2 * CHIPS
     me = lax.axis_index("tp")
@@ -44,7 +47,7 @@
     chip = [(c + o) % CHIPS for o in OFFSET]
     right, left = 2 * chip[RIGHT] + k, 2 * chip[LEFT] + k
     vocab, dim = e_hbm.shape
-    nv, ne = vocab // vc, vocab // ec
+    nv = vocab // vc
 
     def remote(src, dst, send, recv, dev):
         return pltpu.make_async_remote_copy(
@@ -122,7 +125,7 @@
         if h == 0:
             for j in range(1, group):
                 go(tm_copy(j))
-        for i in (TO_PARTNER, TO_RIGHT, TO_LEFT):
+        for i in (TO_PARTNER, TO_RIGHT, TO_LEFT) if h == 0 else (TO_PARTNER,):
             go(ag_copy(h, i))
 
     def tm_arrival(j):
@@ -137,7 +140,7 @@
     for cp in e_copies:
         cp.wait()
 
-    iota = lax.broadcasted_iota(jnp.int32, (SUB, 256), 0).reshape(SUB // 8, 8, 256)
+    iota[...] = lax.broadcasted_iota(jnp.int32, (SUB, 128), 0)
 
     def local_target(h, chip_no):
         halves = [
@@ -145,35 +148,45 @@
         ]
         return jnp.concatenate(halves, axis=1)
 
+    def weights(slot):
+        return de.at[slot] if slot < 2 else w.at[slot - 2]
+
+    def fwd_chunk(rows0, tgt8, slot, s_acc, t_acc):
+        z = jnp.dot(e[pl.ds(rows0, vc), :], xt[...], preferred_element_type=jnp.float32)
+        w_c, vb_c = weights(slot).at[pl.ds(rows0, vc)], vb.at[pl.ds(rows0, vc)]
+        for j in range(vc // SUB):
+            rows = slice(j * SUB, j * SUB + SUB)
+            ok, num = vb_c[rows, :], iota[...]
+            hit = jnp.concatenate([num, num], axis=1).reshape(SUB // 8, 8, 256) == (tgt8 - (rows0 + j * SUB))[None]
+            t = jnp.tanh(z[rows, :] * (1.0 / SOFT_CAP))
+            ex = jnp.exp2(t * EXP_SCALE) * jnp.concatenate([ok, ok], axis=1)
+            w_c[rows, :] = ex * (1.0 - t * t)
+            s_acc = s_acc + jnp.sum(ex.reshape(SUB // 8, 8, 256), axis=0)
+            t_acc = jnp.where(hit, t.reshape(SUB // 8, 8, 256), t_acc)
+        return s_acc, t_acc
+
+    def fwd_begin(h, r):
+        xt[...] = x_all[h, chip[r]].reshape(2 * HT, dim).T
+        return local_target(h, chip[r])
+
+    def fwd_end(h, r, s_acc, t_acc):
+        s_row = jnp.sum(s_acc, axis=0, keepdims=True)
+        t_row = jnp.sum(t_acc.reshape(SUB, 256), axis=0, keepdims=True)
+        for kk in range(2):
+            st_send[h, pl.ds(2 * chip[r] + kk, 1), :] = s_row[:, kk * 128 : (kk + 1) * 128]
+            st_send[h, pl.ds(group + 2 * chip[r] + kk, 1), :] = t_row[:, kk * 128 : (kk + 1) * 128]
+
+    zero = (jnp.zeros((8, 256), jnp.float32), jnp.zeros((SUB // 8, 8, 256), jnp.float32))
+
     def forward(h, r, slot):
-        chip_no = chip[r]
-        xt[...] = x_all[h, chip_no].reshape(2 * HT, dim).T
-        tgt8 = local_target(h, chip_no)
+        tgt8 = fwd_begin(h, r)
 
         def body(i, carry):
-            s_acc, t_acc = carry
-            rows0 = pl.multiple_of(i * vc, vc)
-            z = jnp.dot(e[pl.ds(rows0, vc), :], xt[...], preferred_element_type=jnp.float32)
-            tgt_rel = tgt8 - rows0
-            for j in range(vc // SUB):
-                rows = pl.ds(pl.multiple_of(rows0 + j * SUB, SUB), SUB)
-                ok = vb[rows, :]
-                ok = jnp.concatenate([ok, ok], axis=1)
-                t = jnp.tanh(z[j * SUB : (j + 1) * SUB, :] * (1.0 / SOFT_CAP))
-                ex = jnp.exp2(t * EXP_SCALE) * ok
-                w[slot, rows, :] = ex * (1.0 - t * t)
-                hit = iota == (tgt_rel - j * SUB)[None]
-                s_acc = s_acc + jnp.sum(ex.reshape(SUB // 8, 8, 256), axis=0)
-                t_acc = t_acc + jnp.sum(jnp.where(hit, t.reshape(SUB // 8, 8, 256), 0.0), axis=0)
-            return s_acc, t_acc
-
-        zero = jnp.zeros((8, 256), jnp.float32)
-        s_acc, t_acc = lax.fori_loop(0, nv, body, (zero, zero))
-        s_row = jnp.sum(s_acc, axis=0, keepdims=True)
-        t_row = jnp.sum(t_acc, axis=0, keepdims=True)
-        for kk in range(2):
-            st_send[h, pl.ds(2 * chip_no + kk, 1), :] = s_row[:, kk * 128 : (kk + 1) * 128]
-            st_send[h, pl.ds(group + 2 * chip_no + kk, 1), :] = t_row[:, kk * 128 : (kk + 1) * 128]
+            for u in range(fu):
+                carry = fwd_chunk(pl.multiple_of((i * fu + u) * vc, vc), tgt8, slot, *carry)
+            return carry
+
+        fwd_end(h, r, *lax.fori_loop(0, nv // fu, body, zero))
 
     def st_copy(h, j):
         n = h * (group - 1) + j - 1
@@ -210,29 +223,51 @@
             [jnp.broadcast_to(ref[h, pl.ds(2 * chip_no + kk, 1), :], (8, 128)) for kk in range(2)], axis=1
         )
 
-    def backward(h, r, slot):
-        chip_no = chip[r]
-        tile = h * CHIPS + chip_no
-        tgt8 = local_target(h, chip_no)
-        a8, d8 = spread(av, h, chip_no)[None], spread(dv, h, chip_no)[None]
+    def bwd_begin(h, r):
         for kk in range(2):
             dx[h, r, kk] = jnp.zeros((dim, HT), jnp.float32)
-
-        @pl.loop(0, nv)
+        return local_target(h, chip[r]), spread(av, h, chip[r]), spread(dv, h, chip[r])
+
+    def bwd_chunk(i, h, r, slot, tgt8, a8, d8):
+        rows0 = pl.multiple_of(i * vc, vc)
+        pieces = []
+        w_c, dz_c = weights(slot).at[pl.ds(rows0, vc)], dz.at[h * CHIPS + chip[r], pl.ds(rows0, vc)]
+        for j in range(vc // SUB):
+            rows = slice(j * SUB, j * SUB + SUB)
+            num = iota[...]
+            hit = jnp.concatenate([num, num], axis=1).reshape(SUB // 8, 8, 256) == (tgt8 - (rows0 + j * SUB))[None]
+            g = jnp.where(hit, d8[None], a8[None] * w_c[rows, :].reshape(SUB // 8, 8, 256))
+            g = g.reshape(SUB, 256).astype(jnp.bfloat16)
+            dz_c[rows, :] = g
+            pieces.append(g)
+        return jnp.dot(et[i], jnp.concatenate(pieces, axis=0), preferred_element_type=jnp.float32)
+
+    def bwd_add(h, r, part):
+        for kk in range(2):
+            dx[h, r, kk] += part[:, kk * HT : (kk + 1) * HT]
+
+    def backward(h, r, slot):
+        vecs = bwd_begin(h, r)
+
+        @pl.loop(0, nv // bu)
         def _(i):
-            rows0 = pl.multiple_of(i * vc, vc)
-            tgt_rel = tgt8 - rows0
-            pieces = []
-            for j in range(vc // SUB):
-                rows = pl.ds(pl.multiple_of(rows0 + j * SUB, SUB), SUB)
-                hit = iota == (tgt_rel - j * SUB)[None]
-                g = jnp.where(hit, d8, a8 * w[slot, rows, :].reshape(SUB // 8, 8, 256))
-                g = g.reshape(SUB, 256).astype(jnp.bfloat16)
-                dz[tile, rows, :] = g
-                pieces.append(g)
-            part = jnp.dot(et[i], jnp.concatenate(pieces, axis=0), preferred_element_type=jnp.float32)
-            for kk in range(2):
-                dx[h, r, kk] += part[:, kk * HT : (kk + 1) * HT]
+            part = None
+            for u in range(bu):
+                more = bwd_chunk(i * bu + u, h, r, slot, *vecs)
+                part = more if part is None else part + more
+            bwd_add(h, r, part)
+
+    def both(hb, rb, hf, rf, slot):
+        vecs = bwd_begin(hb, rb)
+        tgt8 = fwd_begin(hf, rf)
+
+        def body(i, carry):
+            part = bwd_chunk(i, hb, rb, slot, *vecs)
+            carry = fwd_chunk(pl.multiple_of(i * vc, vc), tgt8, slot, *carry)
+            bwd_add(hb, rb, part)
+            return carry
+
+        fwd_end(hf, rf, *lax.fori_loop(0, nv, body, zero))
 
     dlo, dhi = pl.ds(0, dim // 2), pl.ds(dim // 2, dim // 2)
 
@@ -278,31 +313,29 @@
         dh_out[h * HT : (h + 1) * HT, :] = (rstd * (dxh - m1 - xh * m2)).astype(jnp.bfloat16)
         return jnp.sum(dn * xh, axis=0, keepdims=True), jnp.sum(dn, axis=0, keepdims=True)
 
-    def out_copy(i, slot):
-        return pltpu.make_async_copy(
-            stage.at[slot], de_hbm.at[pl.ds(pl.multiple_of(i * ec, ec), ec)], out_sem.at[slot]
-        )
-
     def embed(first, last):
         @pl.loop(first, last)
         def _(i):
-            slot = i % 2
-
-            @pl.when(i >= 2)
-            def _():
-                out_copy(i - 2, slot).wait()
-
             rows = pl.ds(pl.multiple_of(i * ec, ec), ec)
-            acc = None
-            for tile in range(2 * CHIPS):
-                xx = x_all[tile // CHIPS, tile % CHIPS].reshape(2 * HT, dim)
-                part = jnp.dot(dz[tile, rows, :], xx, preferred_element_type=jnp.float32)
-                acc = part if acc is None else acc + part
-            stage[slot] = acc
-            out_copy(i, slot).start()
+            acc = embed_rows(dz, x_all, rows)
+            for half in range(2):
+                de[half, rows, :] = acc[:, half * 256 : (half + 1) * 256]
 
     jp = 6 - 6 * k
     ref0 = tm_all.at[0]
+
+    def ag_pass(h):
+        ag_arrival(h, TO_RIGHT)
+        ag_arrival(h, TO_LEFT)
+        for i in (FWD_RIGHT, FWD_LEFT, REL_RIGHT, REL_LEFT):
+            go(ag_copy(h, i))
+
+    def ag_pass_opp(h):
+        ag_arrival(h, FWD_RIGHT)
+        ag_arrival(h, FWD_LEFT)
+        for i in (REL_OPP_A, REL_OPP_B):
+            go(ag_copy(h, i))
+
     remote(ref0, ref0, tm_s.at[jp], tm_r.at[jp], partner).wait_recv()
     ag_arrival(0, TO_PARTNER)
     forward(0, OWN, 0)
@@ -311,81 +344,65 @@
     for i in range(1, group - 1):
         n = (jp + i) % (group - 1)
         remote(ref0, ref0, tm_s.at[n], tm_r.at[n], partner).wait_recv()
-
-    def ag_pass(h):
-        ag_arrival(h, TO_RIGHT)
-        ag_arrival(h, TO_LEFT)
-        for i in (FWD_RIGHT, FWD_LEFT, REL_RIGHT, REL_LEFT):
-            go(ag_copy(h, i))
-
-    def ag_pass_opp(h):
-        ag_arrival(h, FWD_RIGHT)
-        ag_arrival(h, FWD_LEFT)
-        for i in (REL_OPP_A, REL_OPP_B):
-            go(ag_copy(h, i))
-
     ag_pass(0)
+    go(ag_copy(1, TO_RIGHT))
+    go(ag_copy(1, TO_LEFT))
+
+    @pl.loop(0, nv)
+    def _(i):
+        et[i] = e[pl.ds(pl.multiple_of(i * vc, vc), vc), :].T
+
     ag_arrival(0, REL_RIGHT)
     forward(0, RIGHT, 2)
-    ag_pass(1)
+    ag_pass_opp(0)
     ag_arrival(0, REL_LEFT)
     forward(0, LEFT, 3)
-    ag_pass_opp(0)
+    ag_pass(1)
     ag_arrival(0, REL_OPP_A)
     ag_arrival(0, REL_OPP_B)
     forward(0, OPP, 4)
     stats_start(0)
-
-    @pl.loop(0, nv)
-    def _(i):
-        et[i] = e[pl.ds(pl.multiple_of(i * vc, vc), vc), :].T
-
+    ag_arrival(1, REL_RIGHT)
+    forward(1, RIGHT, 5)
     ag_pass_opp(1)
     stats_finish(0)
-    backward(0, OPP, 4)
+    ag_arrival(1, REL_LEFT)
+    both(0, OPP, 1, LEFT, 4)
     pair_start(0, OPP)
-    ag_arrival(1, REL_RIGHT)
-    forward(1, RIGHT, 4)
+    ag_arrival(1, REL_OPP_A)
+    ag_arrival(1, REL_OPP_B)
+    both(0, RIGHT, 1, OPP, 2)
+    stats_start(1)
+    pair_start(0, RIGHT)
     opp_send(0)
-    backward(0, RIGHT, 2)
-    pair_start(0, RIGHT)
-    ag_arrival(1, REL_LEFT)
-    forward(1, LEFT, 2)
-    right_send(0)
     backward(0, LEFT, 3)
     pair_start(0, LEFT)
-    ag_arrival(1, REL_OPP_A)
-    ag_arrival(1, REL_OPP_B)
-    forward(1, OPP, 3)
-    stats_start(1)
-    left_send(0)
-    ring_send(0)
+    right_send(0)
     backward(0, OWN, 0)
     pair_start(0, OWN)
+    left_send(0)
     stats_finish(1)
     loss_out[...] = jnp.concatenate([ls[h, pl.ds(me, 1), :] for h in range(2)], axis=0)
-    both = ls[0] + ls[1]
-    mean_out[...] = jnp.sum(jnp.sum(both, axis=1, keepdims=True), axis=0, keepdims=True) / token_count()
-    backward(1, OPP, 3)
+    total = ls[0] + ls[1]
+    mean_out[...] = jnp.sum(jnp.sum(total, axis=1, keepdims=True), axis=0, keepdims=True) / token_count()
+    backward(1, OPP, 2)
     pair_start(1, OPP)
-    pair_finish(0, OWN)
-    backward(1, RIGHT, 4)
+    ring_send(0)
+    backward(1, RIGHT, 5)
     pair_start(1, RIGHT)
     opp_send(1)
-    backward(1, LEFT, 2)
+    backward(1, LEFT, 4)
     pair_start(1, LEFT)
     right_send(1)
     backward(1, OWN, 1)
     pair_start(1, OWN)
     left_send(1)
-    quarter = ne // 4
-    embed(0, quarter)
+    embed(0, 2)
+    ring_send(1)
+    pair_finish(0, OWN)
     pair_finish(1, OWN)
-    embed(quarter, 2 * quarter)
-    ring_send(1)
-    embed(2 * quarter, 3 * quarter)
     g0, b0 = finish(0)
-    embed(3 * quarter, ne)
+    embed(2, n1)
     g1, b1 = finish(1)
     g, b = g0 + g1, b0 + b1
     for i in range(4):
@@ -397,15 +414,47 @@
 
     for j in range(1, group):
         go(gb_copy(j))
-    for i in range(ne - 2, ne):
-        out_copy(i, i % 2).wait()
+    embed(n1, n2)
     tot = gb_send[...]
     for j in range(1, group):
         gb_copy(j).wait_recv()
         tot = tot + gb_recv[j - 1]
-    gb_out[...] = tot
+    gain_out[...], bias_out[...] = tot[:4], tot[4:]
     for copy in started:
         copy.wait_send()
+
+
+def embed_rows(dz, x_all, rows):
+    acc = None
+    for tile in range(2 * CHIPS):
+        xx = x_all[tile // CHIPS, tile % CHIPS].reshape(2 * HT, -1)
+        part = jnp.dot(dz[tile, rows, :], xx, preferred_element_type=jnp.float32)
+        acc = part if acc is None else acc + part
+    return acc
+
+
+def write_out(
+    de, loss_in, mean_in, dh_in, gain_in, bias_in,
+    loss_out, mean_out, dh_out, de_hbm, gain_out, bias_out,
+    sems, *, pieces,
+):
+    rows = de_hbm.shape[0] // pieces
+    half = de_hbm.shape[1] // 2
+    copies = []
+
+    def go(src, dst):
+        copies.append(pltpu.make_async_copy(src, dst, sems.at[len(copies)]))
+        copies[-1].start()
+
+    for i in range(pieces):
+        part = pl.ds(i * rows, rows)
+        for c in range(2):
+            go(de.at[c, part], de_hbm.at[part, pl.ds(c * half, half)])
+    for src, dst in ((dh_in, dh_out), (loss_in, loss_out), (gain_in, gain_out), (bias_in, bias_out)):
+        go(src, dst)
+    mean_out[...] = mean_in[...]
+    for copy in copies:
+        copy.wait()
 
 
 def solution(mesh):
@@ -416,31 +465,32 @@
         vocab = out_embed.shape[0]
         group = 2 * CHIPS
         assert rows == 2 * HT
-        vc, ec = 1024, 512
+        vc, ec, fu, bu, n1, n2 = CFG
         nv = vocab // vc
         f32, bf16, i32 = jnp.float32, jnp.bfloat16, jnp.int32
         vmem = pl.BlockSpec(memory_space=pltpu.VMEM)
         hbm = pl.BlockSpec(memory_space=pl.ANY)
         dma = pltpu.SemaphoreType.DMA
-        loss, mean, dh, de, gb = pl.pallas_call(
-            functools.partial(kernel, vc=vc, ec=ec),
+        results = pl.pallas_call(
+            functools.partial(kernel, vc=vc, ec=ec, fu=fu, bu=bu, n1=n1, n2=n2),
             out_shape=(
-                jax.ShapeDtypeStruct((2, 128), f32),
-                jax.ShapeDtypeStruct((1, 1), f32),
-                jax.ShapeDtypeStruct((rows, dim), bf16),
-                jax.ShapeDtypeStruct((vocab, dim), f32),
-                jax.ShapeDtypeStruct((8, 128), f32),
+                pltpu.VMEM((2, vocab, dim // 2), f32),
+                pltpu.VMEM((2, 128), f32),
+                pltpu.VMEM((1, 1), f32),
+                pltpu.VMEM((rows, dim), bf16),
+                pltpu.VMEM((4, 128), f32),
+                pltpu.VMEM((4, 128), f32),
             ),
             in_specs=[vmem, vmem, vmem, hbm, vmem, vmem, vmem],
-            out_specs=(vmem, vmem, vmem, hbm, vmem),
+            out_specs=(vmem,) * 6,
             scratch_shapes=[
+                pltpu.VMEM((2 * CHIPS, vocab, 2 * HT), bf16),
                 pltpu.VMEM((2, CHIPS, 2, HT, dim), bf16),
+                pltpu.VMEM((SLOTS - 2, vocab, 2 * HT), f32),
                 pltpu.VMEM((dim, 2 * HT), bf16),
                 pltpu.VMEM((vocab, dim), bf16),
                 pltpu.VMEM((nv, dim, vc), bf16),
                 pltpu.VMEM((vocab, 128), f32),
-                pltpu.VMEM((5, vocab, 2 * HT), f32),
-                pltpu.VMEM((2 * CHIPS, vocab, 2 * HT), bf16),
                 pltpu.VMEM((group, 2, 128), i32),
                 pltpu.VMEM((2, 2 * group, 128), f32),
                 pltpu.VMEM((2, group - 1, 2 * group, 128), f32),
@@ -453,9 +503,8 @@
                 pltpu.VMEM((2, 2, dim, HT), f32),
                 pltpu.VMEM((8, 128), f32),
                 pltpu.VMEM((group - 1, 8, 128), f32),
-                pltpu.VMEM((2, ec, dim), f32),
+                pltpu.VMEM((SUB, 128), i32),
                 dma((nv,)),
-                dma((2,)),
                 dma((group - 1,)),
                 dma((group - 1,)),
                 dma((18,)),
@@ -468,7 +517,7 @@
                 dma((group - 1,)),
             ],
             compiler_params=pltpu.CompilerParams(
-                collective_id=0, has_side_effects=True, vmem_limit_bytes=67043328
+                collective_id=0, has_side_effects=True, vmem_limit_bytes=LIM << 20
             ),
             name="vocab_xent",
         )(
@@ -480,13 +529,29 @@
             targets.reshape(2, 128),
             loss_mask.reshape(2, 128),
         )
+        loss, mean, dh, de, dgain, dbias = pl.pallas_call(
+            functools.partial(write_out, pieces=4),
+            out_shape=(
+                jax.ShapeDtypeStruct((2, 128), f32),
+                jax.ShapeDtypeStruct((1, 1), f32),
+                jax.ShapeDtypeStruct((rows, dim), bf16),
+                jax.ShapeDtypeStruct((vocab, dim), f32),
+                jax.ShapeDtypeStruct((4, 128), f32),
+                jax.ShapeDtypeStruct((4, 128), f32),
+            ),
+            in_specs=[vmem] * 6,
+            out_specs=(hbm, vmem, hbm, hbm, hbm, hbm),
+            scratch_shapes=[dma((12,))],
+            compiler_params=pltpu.CompilerParams(vmem_limit_bytes=2 << 20),
+            name="write_out",
+        )(*results)
         return (
             loss.reshape(rows),
             mean.reshape(1),
             dh,
             de,
-            gb[:4].reshape(dim),
-            gb[4:].reshape(dim),
+            dgain.reshape(dim),
+            dbias.reshape(dim),
         )
 
     row_spec = P(("dp", "tp"))

time: 87.3 us -> 65.9 us (0.75)
  local copies, waits for them, and re-layouts: 11.9 us -> 0 us
  Pallas kernels: 72.7 us -> 65.1 us
  between operations: 2.41 us -> 0.64 us
    unnamed x3 -> x0, local copies, waits for them, and re-layouts: 10.6 us -> none
    pallas_call x1 -> x2, Pallas kernels: 72.7 us -> 65.1 us  [the longest x1 60.5 us: group_step(): pl.pallas_call(functools.partial(kernel, vc=vc, ec=ec, fu=fu, bu=bu, n1=n...]
    reshape x1 -> x0, local copies, waits for them, and re-layouts: 1.33 us -> none  [group_step(): gb[4:].reshape(dim)]
where the time goes in v2:
time: 65.9 us; the launch traced here: 65.8 us
  Pallas kernels  65.1 us (99%)
    pallas_call x1, Pallas kernels, group_step(): pl.pallas_call(functools.partial(kernel, vc=vc, ec=ec, fu=fu, bu=bu, n1=n...  60.5 us
    pallas_call x1, Pallas kernels, group_step(): pl.pallas_call(functools.partial(write_out, pieces=4), out_shape=(jax.Sha...  4.6 us

profile of v2, /device:TPU:113, one launch (start us, length us, event | category | flops | bytes accessed | tf_op | source)
XLA Modules:
  0.0 65.8 jit_solution(11077235493837852235)
XLA Ops:
  0.6 60.5 %vocab_xent.1 = (f32[2,4096,256]{2,1,0:T(8,128)S(1)}, f32[2,128]{1,0:T(2,128)S(1)}, f32[1,1]{1,0:T(1,128)}, bf16[256,512]{1,0:T(8,128)(2,1)S(1)}, f32[4,128]{1,0:T(4,128)S(1)}, /*index=5*/f32[4,128]{1,0:T(4,128)S(1)}) custom-call(bf16[256,512]{1,0:T(8,128)(2,1)} %hid.1, f32[1,512]{1,0:T(1,128)} %bitcast.10, f32[1,512]{1,0:T(1,128)} %bitcast.11, ...), custom_call_target="tpu_custom_call" | custom-call | tf_op jit(solution)/shard_map/vocab_xent/pallas_call | solution.py:474
  61.2 4.6 %write_out.1 = (f32[2,128]{1,0:T(2,128)}, f32[1,1]{1,0:T(1,128)}, bf16[256,512]{1,0:T(8,128)(2,1)}, f32[4096,512]{1,0:T(8,128)}, f32[4,128]{1,0:T(4,128)}, /*index=5*/f32[4,128]{1,0:T(4,128)}) custom-call(f32[2,4096,256]{2,1,0:T(8,128)S(1)} %get-tuple-element.18.de, f32[2,128]{1,0:T(2,128)S(1)} %get-tuple-element.19.loss_in, ...), custom_call_target="tpu_custom_call" | custom-call | tf_op jit(solution)/shard_map/write_out/pallas_call | solution.py:532

commit v3 on v2

--- a/solution.py
+++ b/solution.py
@@ -15,10 +15,12 @@
 CHIPS = 4
 OFFSET = (0, 1, 3, 2)
 OWN, RIGHT, LEFT, OPP = range(4)
+GRADS = ((0, OPP), (0, RIGHT), (0, LEFT), (0, OWN), (1, OPP), (1, RIGHT), (1, LEFT), (1, OWN))
 HT = 128
-CFG = (1024, 512, 1, 1, 6, 8)
+CFG = (512, 512, 6, 8)
+FS, BS, CS = 2048, 2048, 1024
 SLOTS = 6
-LIM = 54
+LIM = 54 * 2**20
 SUB = 32
 
 TO_PARTNER, TO_RIGHT, TO_LEFT, FWD_RIGHT, FWD_LEFT, REL_LEFT, REL_RIGHT, REL_OPP_A, REL_OPP_B = range(9)
@@ -37,7 +39,7 @@
     de, loss_out, mean_out, dh_out, gain_out, bias_out,
     dz, x_all, w, xt, e, et, vb, tm_all, st_send, st_recv, av, dv, ls, dx, d2d, ring, fin, gb_send, gb_recv, iota,
     e_sem, tm_s, tm_r, ag_s, ag_r, st_s, st_r, rs_s, rs_r, gb_s, gb_r,
-    *, vc, ec, fu, bu, n1, n2,
+    *, vc, ec, n1, n2,
 ):
     group = 2 * CHIPS
     me = lax.axis_index("tp")
@@ -125,7 +127,7 @@
         if h == 0:
             for j in range(1, group):
                 go(tm_copy(j))
-        for i in (TO_PARTNER, TO_RIGHT, TO_LEFT) if h == 0 else (TO_PARTNER,):
+        for i in (TO_PARTNER, TO_RIGHT, TO_LEFT):
             go(ag_copy(h, i))
 
     def tm_arrival(j):
@@ -151,42 +153,54 @@
     def weights(slot):
         return de.at[slot] if slot < 2 else w.at[slot - 2]
 
-    def fwd_chunk(rows0, tgt8, slot, s_acc, t_acc):
-        z = jnp.dot(e[pl.ds(rows0, vc), :], xt[...], preferred_element_type=jnp.float32)
-        w_c, vb_c = weights(slot).at[pl.ds(rows0, vc)], vb.at[pl.ds(rows0, vc)]
-        for j in range(vc // SUB):
+    def fwd_begin(tiles):
+        for n, (h, r, _) in enumerate(tiles):
+            xt[:, n * 256 : (n + 1) * 256] = x_all[h, chip[r]].reshape(2 * HT, dim).T
+        return [local_target(h, chip[r]) for h, r, _ in tiles]
+
+    def softmax_part(rows0, size, tgts, tiles, carry):
+        count = len(tiles)
+        z = jnp.dot(e[pl.ds(rows0, size), :], xt[:, : count * 256], preferred_element_type=jnp.float32)
+        vb_c = vb.at[pl.ds(rows0, size)]
+        outs = [weights(slot).at[pl.ds(rows0, size)] for _, _, slot in tiles]
+        carry = list(carry)
+        for j in range(size // SUB):
             rows = slice(j * SUB, j * SUB + SUB)
             ok, num = vb_c[rows, :], iota[...]
-            hit = jnp.concatenate([num, num], axis=1).reshape(SUB // 8, 8, 256) == (tgt8 - (rows0 + j * SUB))[None]
-            t = jnp.tanh(z[rows, :] * (1.0 / SOFT_CAP))
-            ex = jnp.exp2(t * EXP_SCALE) * jnp.concatenate([ok, ok], axis=1)
-            w_c[rows, :] = ex * (1.0 - t * t)
-            s_acc = s_acc + jnp.sum(ex.reshape(SUB // 8, 8, 256), axis=0)
-            t_acc = jnp.where(hit, t.reshape(SUB // 8, 8, 256), t_acc)
-        return s_acc, t_acc
-
-    def fwd_begin(h, r):
-        xt[...] = x_all[h, chip[r]].reshape(2 * HT, dim).T
-        return local_target(h, chip[r])
-
-    def fwd_end(h, r, s_acc, t_acc):
-        s_row = jnp.sum(s_acc, axis=0, keepdims=True)
-        t_row = jnp.sum(t_acc.reshape(SUB, 256), axis=0, keepdims=True)
-        for kk in range(2):
-            st_send[h, pl.ds(2 * chip[r] + kk, 1), :] = s_row[:, kk * 128 : (kk + 1) * 128]
-            st_send[h, pl.ds(group + 2 * chip[r] + kk, 1), :] = t_row[:, kk * 128 : (kk + 1) * 128]
-
-    zero = (jnp.zeros((8, 256), jnp.float32), jnp.zeros((SUB // 8, 8, 256), jnp.float32))
-
-    def forward(h, r, slot):
-        tgt8 = fwd_begin(h, r)
+            ok = jnp.concatenate([ok, ok], axis=1)
+            num = jnp.concatenate([num, num], axis=1).reshape(SUB // 8, 8, 256)
+            for n in range(count):
+                s_acc, t_acc = carry[n]
+                t = jnp.tanh(z[rows, n * 256 : (n + 1) * 256] * (1.0 / SOFT_CAP))
+                ex = jnp.exp2(t * EXP_SCALE) * ok
+                outs[n][rows, :] = ex * (1.0 - t * t)
+                hit = num == (tgts[n] - (rows0 + j * SUB))[None]
+                s_acc = s_acc + jnp.sum(ex.reshape(SUB // 8, 8, 256), axis=0)
+                t_acc = jnp.where(hit, t.reshape(SUB // 8, 8, 256), t_acc)
+                carry[n] = s_acc, t_acc
+        return tuple(carry)
+
+    def fwd_end(tiles, carry):
+        for (h, r, _), (s_acc, t_acc) in zip(tiles, carry):
+            s_row = jnp.sum(s_acc, axis=0, keepdims=True)
+            t_row = jnp.sum(t_acc.reshape(SUB, 256), axis=0, keepdims=True)
+            for kk in range(2):
+                st_send[h, pl.ds(2 * chip[r] + kk, 1), :] = s_row[:, kk * 128 : (kk + 1) * 128]
+                st_send[h, pl.ds(group + 2 * chip[r] + kk, 1), :] = t_row[:, kk * 128 : (kk + 1) * 128]
+
+    def fwd_zero(tiles):
+        zero = (jnp.zeros((8, 256), jnp.float32), jnp.zeros((SUB // 8, 8, 256), jnp.float32))
+        return tuple(zero for _ in tiles)
+
+    def forward(*tiles):
+        size = FS
+        steps = vocab // size
+        tgts = fwd_begin(tiles)
 
         def body(i, carry):
-            for u in range(fu):
-                carry = fwd_chunk(pl.multiple_of((i * fu + u) * vc, vc), tgt8, slot, *carry)
-            return carry
-
-        fwd_end(h, r, *lax.fori_loop(0, nv // fu, body, zero))
+            return softmax_part(pl.multiple_of(i * size, size), size, tgts, tiles, carry)
+
+        fwd_end(tiles, lax.fori_loop(0, steps, body, fwd_zero(tiles)))
 
     def st_copy(h, j):
         n = h * (group - 1) + j - 1
@@ -228,19 +242,29 @@
             dx[h, r, kk] = jnp.zeros((dim, HT), jnp.float32)
         return local_target(h, chip[r]), spread(av, h, chip[r]), spread(dv, h, chip[r])
 
-    def bwd_chunk(i, h, r, slot, tgt8, a8, d8):
-        rows0 = pl.multiple_of(i * vc, vc)
-        pieces = []
-        w_c, dz_c = weights(slot).at[pl.ds(rows0, vc)], dz.at[h * CHIPS + chip[r], pl.ds(rows0, vc)]
-        for j in range(vc // SUB):
-            rows = slice(j * SUB, j * SUB + SUB)
-            num = iota[...]
-            hit = jnp.concatenate([num, num], axis=1).reshape(SUB // 8, 8, 256) == (tgt8 - (rows0 + j * SUB))[None]
-            g = jnp.where(hit, d8[None], a8[None] * w_c[rows, :].reshape(SUB // 8, 8, 256))
-            g = g.reshape(SUB, 256).astype(jnp.bfloat16)
-            dz_c[rows, :] = g
-            pieces.append(g)
-        return jnp.dot(et[i], jnp.concatenate(pieces, axis=0), preferred_element_type=jnp.float32)
+    def grad_store(h, r):
+        n = GRADS.index((h, r))
+        return dz.at[n] if n < 6 else e.at[:, pl.ds((n - 6) * 256, 256)]
+
+    def hidden_part(i, size, h, r, slot, tgt8, a8, d8):
+        rows0 = pl.multiple_of(i * size, size)
+        w_c, dz_c = weights(slot).at[pl.ds(rows0, size)], grad_store(h, r).at[pl.ds(rows0, size)]
+        part = None
+        for u in range(size // vc):
+            pieces = []
+            for j in range(u * vc // SUB, (u + 1) * vc // SUB):
+                rows = slice(j * SUB, j * SUB + SUB)
+                num = iota[...]
+                hit = jnp.concatenate([num, num], axis=1).reshape(SUB // 8, 8, 256) == (tgt8 - (rows0 + j * SUB))[None]
+                g = jnp.where(hit, d8[None], a8[None] * w_c[rows, :].reshape(SUB // 8, 8, 256))
+                g = g.reshape(SUB, 256).astype(jnp.bfloat16)
+                dz_c[rows, :] = g
+                pieces.append(g)
+            more = jnp.dot(
+                et[i * (size // vc) + u], jnp.concatenate(pieces, axis=0), preferred_element_type=jnp.float32
+            )
+            part = more if part is None else part + more
+        return part
 
     def bwd_add(h, r, part):
         for kk in range(2):
@@ -249,25 +273,22 @@
     def backward(h, r, slot):
         vecs = bwd_begin(h, r)
 
-        @pl.loop(0, nv // bu)
+        @pl.loop(0, vocab // BS)
         def _(i):
-            part = None
-            for u in range(bu):
-                more = bwd_chunk(i * bu + u, h, r, slot, *vecs)
-                part = more if part is None else part + more
-            bwd_add(h, r, part)
+            bwd_add(h, r, hidden_part(i, BS, h, r, slot, *vecs))
 
     def both(hb, rb, hf, rf, slot):
+        tile = ((hf, rf, slot),)
         vecs = bwd_begin(hb, rb)
-        tgt8 = fwd_begin(hf, rf)
+        tgts = fwd_begin(tile)
 
         def body(i, carry):
-            part = bwd_chunk(i, hb, rb, slot, *vecs)
-            carry = fwd_chunk(pl.multiple_of(i * vc, vc), tgt8, slot, *carry)
+            part = hidden_part(i, CS, hb, rb, slot, *vecs)
+            carry = softmax_part(pl.multiple_of(i * CS, CS), CS, tgts, tile, carry)
             bwd_add(hb, rb, part)
             return carry
 
-        fwd_end(hf, rf, *lax.fori_loop(0, nv, body, zero))
+        fwd_end(tile, lax.fori_loop(0, vocab // CS, body, fwd_zero(tile)))
 
     dlo, dhi = pl.ds(0, dim // 2), pl.ds(dim // 2, dim // 2)
 
@@ -313,11 +334,20 @@
         dh_out[h * HT : (h + 1) * HT, :] = (rstd * (dxh - m1 - xh * m2)).astype(jnp.bfloat16)
         return jnp.sum(dn * xh, axis=0, keepdims=True), jnp.sum(dn, axis=0, keepdims=True)
 
+    def embed_rows(rows):
+        acc = None
+        for h in range(2):
+            for r in range(CHIPS):
+                xx = x_all[h, chip[r]].reshape(2 * HT, dim)
+                part = jnp.dot(grad_store(h, r)[rows, :], xx, preferred_element_type=jnp.float32)
+                acc = part if acc is None else acc + part
+        return acc
+
     def embed(first, last):
         @pl.loop(first, last)
         def _(i):
             rows = pl.ds(pl.multiple_of(i * ec, ec), ec)
-            acc = embed_rows(dz, x_all, rows)
+            acc = embed_rows(rows)
             for half in range(2):
                 de[half, rows, :] = acc[:, half * 256 : (half + 1) * 256]
 
@@ -338,33 +368,31 @@
 
     remote(ref0, ref0, tm_s.at[jp], tm_r.at[jp], partner).wait_recv()
     ag_arrival(0, TO_PARTNER)
-    forward(0, OWN, 0)
     ag_arrival(1, TO_PARTNER)
-    forward(1, OWN, 1)
+    forward((0, OWN, 0))
+    forward((1, OWN, 1))
     for i in range(1, group - 1):
         n = (jp + i) % (group - 1)
         remote(ref0, ref0, tm_s.at[n], tm_r.at[n], partner).wait_recv()
     ag_pass(0)
-    go(ag_copy(1, TO_RIGHT))
-    go(ag_copy(1, TO_LEFT))
 
     @pl.loop(0, nv)
     def _(i):
         et[i] = e[pl.ds(pl.multiple_of(i * vc, vc), vc), :].T
 
     ag_arrival(0, REL_RIGHT)
-    forward(0, RIGHT, 2)
+    forward((0, RIGHT, 2))
+    ag_pass(1)
     ag_pass_opp(0)
     ag_arrival(0, REL_LEFT)
-    forward(0, LEFT, 3)
-    ag_pass(1)
+    forward((0, LEFT, 3))
     ag_arrival(0, REL_OPP_A)
     ag_arrival(0, REL_OPP_B)
-    forward(0, OPP, 4)
+    forward((0, OPP, 4))
     stats_start(0)
+    ag_pass_opp(1)
     ag_arrival(1, REL_RIGHT)
-    forward(1, RIGHT, 5)
-    ag_pass_opp(1)
+    forward((1, RIGHT, 5))
     stats_finish(0)
     ag_arrival(1, REL_LEFT)
     both(0, OPP, 1, LEFT, 4)
@@ -424,15 +452,6 @@
         copy.wait_send()
 
 
-def embed_rows(dz, x_all, rows):
-    acc = None
-    for tile in range(2 * CHIPS):
-        xx = x_all[tile // CHIPS, tile % CHIPS].reshape(2 * HT, -1)
-        part = jnp.dot(dz[tile, rows, :], xx, preferred_element_type=jnp.float32)
-        acc = part if acc is None else acc + part
-    return acc
-
-
 def write_out(
     de, loss_in, mean_in, dh_in, gain_in, bias_in,
     loss_out, mean_out, dh_out, de_hbm, gain_out, bias_out,
@@ -465,14 +484,14 @@
         vocab = out_embed.shape[0]
         group = 2 * CHIPS
         assert rows == 2 * HT
-        vc, ec, fu, bu, n1, n2 = CFG
+        vc, ec, n1, n2 = CFG
         nv = vocab // vc
         f32, bf16, i32 = jnp.float32, jnp.bfloat16, jnp.int32
         vmem = pl.BlockSpec(memory_space=pltpu.VMEM)
         hbm = pl.BlockSpec(memory_space=pl.ANY)
         dma = pltpu.SemaphoreType.DMA
         results = pl.pallas_call(
-            functools.partial(kernel, vc=vc, ec=ec, fu=fu, bu=bu, n1=n1, n2=n2),
+            functools.partial(kernel, vc=vc, ec=ec, n1=n1, n2=n2),
             out_shape=(
                 pltpu.VMEM((2, vocab, dim // 2), f32),
                 pltpu.VMEM((2, 128), f32),
@@ -484,7 +503,7 @@
             in_specs=[vmem, vmem, vmem, hbm, vmem, vmem, vmem],
             out_specs=(vmem,) * 6,
             scratch_shapes=[
-                pltpu.VMEM((2 * CHIPS, vocab, 2 * HT), bf16),
+                pltpu.VMEM((6, vocab, 2 * HT), bf16),
                 pltpu.VMEM((2, CHIPS, 2, HT, dim), bf16),
                 pltpu.VMEM((SLOTS - 2, vocab, 2 * HT), f32),
                 pltpu.VMEM((dim, 2 * HT), bf16),
@@ -517,7 +536,7 @@
                 dma((group - 1,)),
             ],
             compiler_params=pltpu.CompilerParams(
-                collective_id=0, has_side_effects=True, vmem_limit_bytes=LIM << 20
+                collective_id=0, has_side_effects=True, vmem_limit_bytes=LIM
             ),
             name="vocab_xent",
         )(

time: 65.9 us -> 63.6 us (0.965)
  Pallas kernels: 65.1 us -> 62.7 us
    pallas_call x1, Pallas kernels: 60.5 us -> 58.1 us  [group_step(): pl.pallas_call(functools.partial(kernel, vc=vc, ec=ec, n1=n1, n2=n2), out...]
where the time goes in v3:
time: 63.6 us; the launch traced here: 63.5 us
  Pallas kernels  62.7 us (99%)
  between operations  0.8 us (1%)
    pallas_call x1, Pallas kernels, group_step(): pl.pallas_call(functools.partial(kernel, vc=vc, ec=ec, n1=n1, n2=n2), out...  58.1 us
    pallas_call x1, Pallas kernels, group_step(): pl.pallas_call(functools.partial(write_out, pieces=4), out_shape=(jax.Sha...  4.6 us

profile of v3, /device:TPU:113, one launch (start us, length us, event | category | flops | bytes accessed | tf_op | source)
XLA Modules:
  0.0 63.5 jit_solution(14828212627547274130)
XLA Ops:
  0.6 58.1 %vocab_xent.1 = (f32[2,4096,256]{2,1,0:T(8,128)S(1)}, f32[2,128]{1,0:T(2,128)S(1)}, f32[1,1]{1,0:T(1,128)}, bf16[256,512]{1,0:T(8,128)(2,1)S(1)}, f32[4,128]{1,0:T(4,128)S(1)}, /*index=5*/f32[4,128]{1,0:T(4,128)S(1)}) custom-call(bf16[256,512]{1,0:T(8,128)(2,1)} %hid.1, f32[1,512]{1,0:T(1,128)} %bitcast.10, f32[1,512]{1,0:T(1,128)} %bitcast.11, ...), custom_call_target="tpu_custom_call" | custom-call | tf_op jit(solution)/shard_map/vocab_xent/pallas_call | solution.py:493
  58.8 4.6 %write_out.1 = (f32[2,128]{1,0:T(2,128)}, f32[1,1]{1,0:T(1,128)}, bf16[256,512]{1,0:T(8,128)(2,1)}, f32[4096,512]{1,0:T(8,128)}, f32[4,128]{1,0:T(4,128)}, /*index=5*/f32[4,128]{1,0:T(4,128)}) custom-call(f32[2,4096,256]{2,1,0:T(8,128)S(1)} %get-tuple-element.18.de, f32[2,128]{1,0:T(2,128)S(1)} %get-tuple-element.19.loss_in, ...), custom_call_target="tpu_custom_call" | custom-call | tf_op jit(solution)/shard_map/write_out/pallas_call | solution.py:551

commit v4 on v3

--- a/solution.py
+++ b/solution.py
@@ -18,7 +18,7 @@
 GRADS = ((0, OPP), (0, RIGHT), (0, LEFT), (0, OWN), (1, OPP), (1, RIGHT), (1, LEFT), (1, OWN))
 HT = 128
 CFG = (512, 512, 6, 8)
-FS, BS, CS = 2048, 2048, 1024
+FS, BS = 2048, 2048
 SLOTS = 6
 LIM = 54 * 2**20
 SUB = 32
@@ -151,7 +151,7 @@
         return jnp.concatenate(halves, axis=1)
 
     def weights(slot):
-        return de.at[slot] if slot < 2 else w.at[slot - 2]
+        return de.at[:, pl.ds(slot * 256, 256)] if slot < 2 else w.at[slot - 2]
 
     def fwd_begin(tiles):
         for n, (h, r, _) in enumerate(tiles):
@@ -277,19 +277,6 @@
         def _(i):
             bwd_add(h, r, hidden_part(i, BS, h, r, slot, *vecs))
 
-    def both(hb, rb, hf, rf, slot):
-        tile = ((hf, rf, slot),)
-        vecs = bwd_begin(hb, rb)
-        tgts = fwd_begin(tile)
-
-        def body(i, carry):
-            part = hidden_part(i, CS, hb, rb, slot, *vecs)
-            carry = softmax_part(pl.multiple_of(i * CS, CS), CS, tgts, tile, carry)
-            bwd_add(hb, rb, part)
-            return carry
-
-        fwd_end(tile, lax.fori_loop(0, vocab // CS, body, fwd_zero(tile)))
-
     dlo, dhi = pl.ds(0, dim // 2), pl.ds(dim // 2, dim // 2)
 
     def rs(h, i, src, dst, dev):
@@ -315,10 +302,12 @@
         pair_finish(h, LEFT)
         go(rs(h, LEFT_LO, dx.at[h, LEFT, k, dlo], fin.at[h, 1, dlo], left))
 
-    def ring_send(h):
+    def ring_right(h):
         rs(h, OPP_RIGHT, ring.at[h, 0], ring.at[h, 0], partner).wait_recv()
         dx[h, RIGHT, k, dlo] = dx[h, RIGHT, k, dlo] + ring[h, 0]
         go(rs(h, RIGHT_LO, dx.at[h, RIGHT, k, dlo], fin.at[h, 0, dlo], right))
+
+    def ring_left(h):
         rs(h, OPP_LEFT, ring.at[h, 1], ring.at[h, 1], partner).wait_recv()
         dx[h, LEFT, k, dhi] = dx[h, LEFT, k, dhi] + ring[h, 1]
         go(rs(h, LEFT_HI, dx.at[h, LEFT, k, dhi], fin.at[h, 1, dhi], left))
@@ -347,9 +336,7 @@
         @pl.loop(first, last)
         def _(i):
             rows = pl.ds(pl.multiple_of(i * ec, ec), ec)
-            acc = embed_rows(rows)
-            for half in range(2):
-                de[half, rows, :] = acc[:, half * 256 : (half + 1) * 256]
+            de[rows, :] = embed_rows(rows)
 
     jp = 6 - 6 * k
     ref0 = tm_all.at[0]
@@ -395,27 +382,30 @@
     forward((1, RIGHT, 5))
     stats_finish(0)
     ag_arrival(1, REL_LEFT)
-    both(0, OPP, 1, LEFT, 4)
+    backward(0, OPP, 4)
     pair_start(0, OPP)
+    backward(0, RIGHT, 2)
+    pair_start(0, RIGHT)
+    opp_send(0)
+    forward((1, LEFT, 4))
+    right_send(0)
     ag_arrival(1, REL_OPP_A)
     ag_arrival(1, REL_OPP_B)
-    both(0, RIGHT, 1, OPP, 2)
+    forward((1, OPP, 2))
     stats_start(1)
-    pair_start(0, RIGHT)
-    opp_send(0)
     backward(0, LEFT, 3)
     pair_start(0, LEFT)
-    right_send(0)
+    ring_right(0)
     backward(0, OWN, 0)
     pair_start(0, OWN)
     left_send(0)
+    ring_left(0)
     stats_finish(1)
     loss_out[...] = jnp.concatenate([ls[h, pl.ds(me, 1), :] for h in range(2)], axis=0)
     total = ls[0] + ls[1]
     mean_out[...] = jnp.sum(jnp.sum(total, axis=1, keepdims=True), axis=0, keepdims=True) / token_count()
     backward(1, OPP, 2)
     pair_start(1, OPP)
-    ring_send(0)
     backward(1, RIGHT, 5)
     pair_start(1, RIGHT)
     opp_send(1)
@@ -426,7 +416,8 @@
     pair_start(1, OWN)
     left_send(1)
     embed(0, 2)
-    ring_send(1)
+    ring_right(1)
+    ring_left(1)
     pair_finish(0, OWN)
     pair_finish(1, OWN)
     g0, b0 = finish(0)
@@ -458,7 +449,6 @@
     sems, *, pieces,
 ):
     rows = de_hbm.shape[0] // pieces
-    half = de_hbm.shape[1] // 2
     copies = []
 
     def go(src, dst):
@@ -467,8 +457,7 @@
 
     for i in range(pieces):
         part = pl.ds(i * rows, rows)
-        for c in range(2):
-            go(de.at[c, part], de_hbm.at[part, pl.ds(c * half, half)])
+        go(de.at[part], de_hbm.at[part])
     for src, dst in ((dh_in, dh_out), (loss_in, loss_out), (gain_in, gain_out), (bias_in, bias_out)):
         go(src, dst)
     mean_out[...] = mean_in[...]
@@ -493,7 +482,7 @@
         results = pl.pallas_call(
             functools.partial(kernel, vc=vc, ec=ec, n1=n1, n2=n2),
             out_shape=(
-                pltpu.VMEM((2, vocab, dim // 2), f32),
+                pltpu.VMEM((vocab, dim), f32),
                 pltpu.VMEM((2, 128), f32),
                 pltpu.VMEM((1, 1), f32),
                 pltpu.VMEM((rows, dim), bf16),
@@ -549,7 +538,7 @@
             loss_mask.reshape(2, 128),
         )
         loss, mean, dh, de, dgain, dbias = pl.pallas_call(
-            functools.partial(write_out, pieces=4),
+            functools.partial(write_out, pieces=8),
             out_shape=(
                 jax.ShapeDtypeStruct((2, 128), f32),
                 jax.ShapeDtypeStruct((1, 1), f32),

time: 63.6 us -> 64.3 us (1.011)
  Pallas kernels: 62.7 us -> 63.4 us
    pallas_call x1, Pallas kernels: 58.1 us -> 58.8 us  [group_step(): pl.pallas_call(functools.partial(kernel, vc=vc, ec=ec, n1=n1, n2=n2), out...]
where the time goes in v4:
time: 64.3 us; the launch traced here: 64.2 us
  Pallas kernels  63.4 us (99%)
  between operations  0.8 us (1%)
    pallas_call x1, Pallas kernels, group_step(): pl.pallas_call(functools.partial(kernel, vc=vc, ec=ec, n1=n1, n2=n2), out...  58.8 us
    pallas_call x1, Pallas kernels, group_step(): pl.pallas_call(functools.partial(write_out, pieces=8), out_shape=(jax.Sha...  4.6 us

profile of v4, /device:TPU:113, one launch (start us, length us, event | category | flops | bytes accessed | tf_op | source)
XLA Modules:
  0.0 64.2 jit_solution(11885039480036850519)
XLA Ops:
  0.6 58.8 %vocab_xent.1 = (f32[4096,512]{1,0:T(8,128)S(1)}, f32[2,128]{1,0:T(2,128)S(1)}, f32[1,1]{1,0:T(1,128)}, bf16[256,512]{1,0:T(8,128)(2,1)S(1)}, f32[4,128]{1,0:T(4,128)S(1)}, /*index=5*/f32[4,128]{1,0:T(4,128)S(1)}) custom-call(bf16[256,512]{1,0:T(8,128)(2,1)} %hid.1, f32[1,512]{1,0:T(1,128)} %bitcast.10, f32[1,512]{1,0:T(1,128)} %bitcast.11, ...), custom_call_target="tpu_custom_call" | custom-call | tf_op jit(solution)/shard_map/vocab_xent/pallas_call | solution.py:482
  59.4 4.6 %write_out.1 = (f32[2,128]{1,0:T(2,128)}, f32[1,1]{1,0:T(1,128)}, bf16[256,512]{1,0:T(8,128)(2,1)}, f32[4096,512]{1,0:T(8,128)}, f32[4,128]{1,0:T(4,128)}, /*index=5*/f32[4,128]{1,0:T(4,128)}) custom-call(f32[4096,512]{1,0:T(8,128)S(1)} %get-tuple-element.18.de, f32[2,128]{1,0:T(2,128)S(1)} %get-tuple-element.19.loss_in, f32[1,1]{1,0:T(1,128)} %get-tuple-element.20.mean_in, ...), custom_call_target="tpu_custom_call" | custom-call | tf_op jit(solution)/shard_map/write_out/pallas_call | solution.py:540

commit v5 on v4

--- a/solution.py
+++ b/solution.py
@@ -17,8 +17,8 @@
 OWN, RIGHT, LEFT, OPP = range(4)
 GRADS = ((0, OPP), (0, RIGHT), (0, LEFT), (0, OWN), (1, OPP), (1, RIGHT), (1, LEFT), (1, OWN))
 HT = 128
-CFG = (512, 512, 6, 8)
-FS, BS = 2048, 2048
+CFG = (512, 512, 5, 8)
+FS, FD, BS, DOT = 2048, 2048, 2048, 128
 SLOTS = 6
 LIM = 54 * 2**20
 SUB = 32
@@ -35,8 +35,9 @@
 
 
 def kernel(
-    hid, gain, bias, e_hbm, valid, tgt, msk,
-    de, loss_out, mean_out, dh_out, gain_out, bias_out,
+    hid_hbm, gain_hbm, bias_hbm, e_hbm, valid_hbm, tgt_hbm, msk_hbm,
+    de, loss_out, dh_out, gain_out, bias_out,
+    hid, gain, bias, valid, tgt, msk, in_sem,
     dz, x_all, w, xt, e, et, vb, tm_all, st_send, st_recv, av, dv, ls, dx, d2d, ring, fin, gb_send, gb_recv, iota,
     e_sem, tm_s, tm_r, ag_s, ag_r, st_s, st_r, rs_s, rs_r, gb_s, gb_r,
     *, vc, ec, n1, n2,
@@ -56,15 +57,22 @@
             src_ref=src, dst_ref=dst, send_sem=send, recv_sem=recv, device_id={"tp": dev}, device_id_type=MESH
         )
 
+    barrier = pltpu.get_barrier_semaphore()
+    for j in range(1, group):
+        pl.semaphore_signal(barrier, inc=1, device_id={"tp": (me + j) % group}, device_id_type=MESH)
+
+    pairs = ((hid_hbm, hid), (gain_hbm, gain), (bias_hbm, bias), (tgt_hbm, tgt), (msk_hbm, msk), (valid_hbm, valid))
+    inputs = [pltpu.make_async_copy(src, dst, in_sem.at[i]) for i, (src, dst) in enumerate(pairs)]
+    for cp in inputs:
+        cp.start()
     e_copies = [
         pltpu.make_async_copy(e_hbm.at[pl.ds(i * vc, vc)], e.at[pl.ds(i * vc, vc)], e_sem.at[i]) for i in range(nv)
     ]
     for cp in e_copies:
         cp.start()
 
-    barrier = pltpu.get_barrier_semaphore()
-    for j in range(1, group):
-        pl.semaphore_signal(barrier, inc=1, device_id={"tp": (me + j) % group}, device_id_type=MESH)
+    for cp in inputs[:5]:
+        cp.wait()
 
     for h in range(2):
         xh, _ = norm(hid[h * HT : (h + 1) * HT, :].astype(jnp.float32))
@@ -116,9 +124,9 @@
 
     started = []
 
-    def go(copy):
-        copy.start()
-        started.append(copy)
+    def go(make, *args):
+        make(*args).start()
+        started.append((make, args))
 
     def tm_copy(j):
         return remote(tm_all.at[me], tm_all.at[me], tm_s.at[j - 1], tm_r.at[j - 1], (me + j) % group)
@@ -126,13 +134,15 @@
     for h in range(2):
         if h == 0:
             for j in range(1, group):
-                go(tm_copy(j))
+                go(tm_copy, j)
         for i in (TO_PARTNER, TO_RIGHT, TO_LEFT):
-            go(ag_copy(h, i))
+            go(ag_copy, h, i)
 
     def tm_arrival(j):
         ref = tm_all.at[(me - j + group) % group]
         remote(ref, ref, tm_s.at[j - 1], tm_r.at[j - 1], partner).wait_recv()
+
+    inputs[5].wait()
 
     @pl.loop(0, vocab // 128)
     def _(i):
@@ -160,18 +170,23 @@
 
     def softmax_part(rows0, size, tgts, tiles, carry):
         count = len(tiles)
-        z = jnp.dot(e[pl.ds(rows0, size), :], xt[:, : count * 256], preferred_element_type=jnp.float32)
+        e_c = e.at[pl.ds(rows0, size)]
         vb_c = vb.at[pl.ds(rows0, size)]
         outs = [weights(slot).at[pl.ds(rows0, size)] for _, _, slot in tiles]
         carry = list(carry)
         for j in range(size // SUB):
+            if j % (DOT // SUB) == 0:
+                z = jnp.dot(
+                    e_c[j * SUB : j * SUB + DOT, :], xt[:, : count * 256], preferred_element_type=jnp.float32
+                )
             rows = slice(j * SUB, j * SUB + SUB)
+            part = slice(j * SUB % DOT, j * SUB % DOT + SUB)
             ok, num = vb_c[rows, :], iota[...]
             ok = jnp.concatenate([ok, ok], axis=1)
             num = jnp.concatenate([num, num], axis=1).reshape(SUB // 8, 8, 256)
             for n in range(count):
                 s_acc, t_acc = carry[n]
-                t = jnp.tanh(z[rows, n * 256 : (n + 1) * 256] * (1.0 / SOFT_CAP))
+                t = jnp.tanh(z[part, n * 256 : (n + 1) * 256] * (1.0 / SOFT_CAP))
                 ex = jnp.exp2(t * EXP_SCALE) * ok
                 outs[n][rows, :] = ex * (1.0 - t * t)
                 hit = num == (tgts[n] - (rows0 + j * SUB))[None]
@@ -192,12 +207,18 @@
         zero = (jnp.zeros((8, 256), jnp.float32), jnp.zeros((SUB // 8, 8, 256), jnp.float32))
         return tuple(zero for _ in tiles)
 
-    def forward(*tiles):
-        size = FS
+    def forward(*tiles, halfway=None):
+        size = FS if len(tiles) == 1 else FD
         steps = vocab // size
         tgts = fwd_begin(tiles)
 
         def body(i, carry):
+            if halfway is not None:
+
+                @pl.when(i == steps // 2)
+                def _():
+                    halfway()
+
             return softmax_part(pl.multiple_of(i * size, size), size, tgts, tiles, carry)
 
         fwd_end(tiles, lax.fori_loop(0, steps, body, fwd_zero(tiles)))
@@ -208,7 +229,7 @@
 
     def stats_start(h):
         for j in range(1, group):
-            go(st_copy(h, j))
+            go(st_copy, h, j)
 
     def token_count():
         total = jnp.zeros((2, 128), jnp.int32)
@@ -283,7 +304,7 @@
         return remote(src, dst, rs_s.at[h * 10 + i], rs_r.at[h * 10 + i], dev)
 
     def pair_start(h, r):
-        go(rs(h, PAIR + r, dx.at[h, r, other], d2d.at[h, r], partner))
+        go(lambda: rs(h, PAIR + r, dx.at[h, r, other], d2d.at[h, r], partner))
 
     def pair_finish(h, r):
         rs(h, PAIR + r, d2d.at[h, r], d2d.at[h, r], partner).wait_recv()
@@ -291,26 +312,26 @@
 
     def opp_send(h):
         pair_finish(h, OPP)
-        go(rs(h, OPP_RIGHT, dx.at[h, OPP, k, dlo], ring.at[h, 0], right))
-        go(rs(h, OPP_LEFT, dx.at[h, OPP, k, dhi], ring.at[h, 1], left))
+        go(lambda: rs(h, OPP_RIGHT, dx.at[h, OPP, k, dlo], ring.at[h, 0], right))
+        go(lambda: rs(h, OPP_LEFT, dx.at[h, OPP, k, dhi], ring.at[h, 1], left))
 
     def right_send(h):
         pair_finish(h, RIGHT)
-        go(rs(h, RIGHT_HI, dx.at[h, RIGHT, k, dhi], fin.at[h, 0, dhi], right))
+        go(lambda: rs(h, RIGHT_HI, dx.at[h, RIGHT, k, dhi], fin.at[h, 0, dhi], right))
 
     def left_send(h):
         pair_finish(h, LEFT)
-        go(rs(h, LEFT_LO, dx.at[h, LEFT, k, dlo], fin.at[h, 1, dlo], left))
+        go(lambda: rs(h, LEFT_LO, dx.at[h, LEFT, k, dlo], fin.at[h, 1, dlo], left))
 
     def ring_right(h):
         rs(h, OPP_RIGHT, ring.at[h, 0], ring.at[h, 0], partner).wait_recv()
         dx[h, RIGHT, k, dlo] = dx[h, RIGHT, k, dlo] + ring[h, 0]
-        go(rs(h, RIGHT_LO, dx.at[h, RIGHT, k, dlo], fin.at[h, 0, dlo], right))
+        go(lambda: rs(h, RIGHT_LO, dx.at[h, RIGHT, k, dlo], fin.at[h, 0, dlo], right))
 
     def ring_left(h):
         rs(h, OPP_LEFT, ring.at[h, 1], ring.at[h, 1], partner).wait_recv()
         dx[h, LEFT, k, dhi] = dx[h, LEFT, k, dhi] + ring[h, 1]
-        go(rs(h, LEFT_HI, dx.at[h, LEFT, k, dhi], fin.at[h, 1, dhi], left))
+        go(lambda: rs(h, LEFT_HI, dx.at[h, LEFT, k, dhi], fin.at[h, 1, dhi], left))
 
     def finish(h):
         for i, n, part in ((RIGHT_HI, 0, dhi), (RIGHT_LO, 0, dlo), (LEFT_LO, 1, dlo), (LEFT_HI, 1, dhi)):
@@ -345,19 +366,18 @@
         ag_arrival(h, TO_RIGHT)
         ag_arrival(h, TO_LEFT)
         for i in (FWD_RIGHT, FWD_LEFT, REL_RIGHT, REL_LEFT):
-            go(ag_copy(h, i))
+            go(ag_copy, h, i)
 
     def ag_pass_opp(h):
         ag_arrival(h, FWD_RIGHT)
         ag_arrival(h, FWD_LEFT)
         for i in (REL_OPP_A, REL_OPP_B):
-            go(ag_copy(h, i))
+            go(ag_copy, h, i)
 
     remote(ref0, ref0, tm_s.at[jp], tm_r.at[jp], partner).wait_recv()
     ag_arrival(0, TO_PARTNER)
     ag_arrival(1, TO_PARTNER)
-    forward((0, OWN, 0))
-    forward((1, OWN, 1))
+    forward((0, OWN, 0), (1, OWN, 1))
     for i in range(1, group - 1):
         n = (jp + i) % (group - 1)
         remote(ref0, ref0, tm_s.at[n], tm_r.at[n], partner).wait_recv()
@@ -387,11 +407,9 @@
     backward(0, RIGHT, 2)
     pair_start(0, RIGHT)
     opp_send(0)
-    forward((1, LEFT, 4))
-    right_send(0)
     ag_arrival(1, REL_OPP_A)
     ag_arrival(1, REL_OPP_B)
-    forward((1, OPP, 2))
+    forward((1, LEFT, 4), (1, OPP, 2), halfway=lambda: right_send(0))
     stats_start(1)
     backward(0, LEFT, 3)
     pair_start(0, LEFT)
@@ -401,9 +419,11 @@
     left_send(0)
     ring_left(0)
     stats_finish(1)
-    loss_out[...] = jnp.concatenate([ls[h, pl.ds(me, 1), :] for h in range(2)], axis=0)
+    for h in range(2):
+        loss_out[h : h + 1, :] = ls[h, pl.ds(me, 1), :]
     total = ls[0] + ls[1]
-    mean_out[...] = jnp.sum(jnp.sum(total, axis=1, keepdims=True), axis=0, keepdims=True) / token_count()
+    mean = jnp.sum(jnp.sum(total, axis=1, keepdims=True), axis=0, keepdims=True) / token_count()
+    loss_out[2:, :] = jnp.broadcast_to(mean, (6, 128))
     backward(1, OPP, 2)
     pair_start(1, OPP)
     backward(1, RIGHT, 5)
@@ -432,21 +452,21 @@
         return remote(gb_send, gb_recv.at[j - 1], gb_s.at[j - 1], gb_r.at[j - 1], (me + j) % group)
 
     for j in range(1, group):
-        go(gb_copy(j))
+        go(gb_copy, j)
     embed(n1, n2)
     tot = gb_send[...]
     for j in range(1, group):
         gb_copy(j).wait_recv()
         tot = tot + gb_recv[j - 1]
     gain_out[...], bias_out[...] = tot[:4], tot[4:]
-    for copy in started:
-        copy.wait_send()
+    for make, args in started:
+        make(*args).wait_send()
 
 
 def write_out(
-    de, loss_in, mean_in, dh_in, gain_in, bias_in,
+    de, loss_in, dh_in, gain_in, bias_in,
     loss_out, mean_out, dh_out, de_hbm, gain_out, bias_out,
-    sems, *, pieces,
+    loss, mean, sems, *, pieces,
 ):
     rows = de_hbm.shape[0] // pieces
     copies = []
@@ -458,9 +478,10 @@
     for i in range(pieces):
         part = pl.ds(i * rows, rows)
         go(de.at[part], de_hbm.at[part])
-    for src, dst in ((dh_in, dh_out), (loss_in, loss_out), (gain_in, gain_out), (bias_in, bias_out)):
+    loss[...] = loss_in[0:2, :]
+    mean[...] = loss_in[2:3, 0:1]
+    for src, dst in ((dh_in, dh_out), (gain_in, gain_out), (bias_in, bias_out), (loss, loss_out), (mean, mean_out)):
         go(src, dst)
-    mean_out[...] = mean_in[...]
     for copy in copies:
         copy.wait()
 
@@ -483,19 +504,25 @@
             functools.partial(kernel, vc=vc, ec=ec, n1=n1, n2=n2),
             out_shape=(
                 pltpu.VMEM((vocab, dim), f32),
-                pltpu.VMEM((2, 128), f32),
-                pltpu.VMEM((1, 1), f32),
+                pltpu.VMEM((8, 128), f32),
                 pltpu.VMEM((rows, dim), bf16),
                 pltpu.VMEM((4, 128), f32),
                 pltpu.VMEM((4, 128), f32),
             ),
-            in_specs=[vmem, vmem, vmem, hbm, vmem, vmem, vmem],
-            out_specs=(vmem,) * 6,
+            in_specs=[hbm] * 7,
+            out_specs=(vmem,) * 5,
             scratch_shapes=[
+                pltpu.VMEM((rows, dim), bf16),
+                pltpu.VMEM((1, dim), f32),
+                pltpu.VMEM((1, dim), f32),
+                pltpu.VMEM((vocab // 128, 128), i32),
+                pltpu.VMEM((2, 128), i32),
+                pltpu.VMEM((2, 128), i32),
+                dma((6,)),
                 pltpu.VMEM((6, vocab, 2 * HT), bf16),
                 pltpu.VMEM((2, CHIPS, 2, HT, dim), bf16),
                 pltpu.VMEM((SLOTS - 2, vocab, 2 * HT), f32),
-                pltpu.VMEM((dim, 2 * HT), bf16),
+                pltpu.VMEM((dim, 4 * HT), bf16),
                 pltpu.VMEM((vocab, dim), bf16),
                 pltpu.VMEM((nv, dim, vc), bf16),
                 pltpu.VMEM((vocab, 128), f32),
@@ -547,9 +574,9 @@
                 jax.ShapeDtypeStruct((4, 128), f32),
                 jax.ShapeDtypeStruct((4, 128), f32),
             ),
-            in_specs=[vmem] * 6,
-            out_specs=(hbm, vmem, hbm, hbm, hbm, hbm),
-            scratch_shapes=[dma((12,))],
+            in_specs=[vmem] * 5,
+            out_specs=(hbm,) * 6,
+            scratch_shapes=[pltpu.VMEM((2, 128), f32), pltpu.VMEM((1, 1), f32), dma((13,))],
             compiler_params=pltpu.CompilerParams(vmem_limit_bytes=2 << 20),
             name="write_out",
         )(*results)

time: 64.3 us -> 63.2 us (0.983)
  Pallas kernels: 63.4 us -> 62.3 us
    pallas_call x1, Pallas kernels: 4.6 us -> 3.47 us  [group_step(): pl.pallas_call(functools.partial(write_out, pieces=8), out_shape=(jax.Sha...]
where the time goes in v5:
time: 63.2 us
  Pallas kernels  62.3 us (99%)
  between operations  0.8 us (1%)
    pallas_call x1, Pallas kernels, group_step(): pl.pallas_call(functools.partial(kernel, vc=vc, ec=ec, n1=n1, n2=n2), out...  58.9 us
    pallas_call x1, Pallas kernels, group_step(): pl.pallas_call(functools.partial(write_out, pieces=8), out_shape=(jax.Sha...  3.47 us

profile of v5, /device:TPU:113, one launch (start us, length us, event | category | flops | bytes accessed | tf_op | source)
XLA Modules:
  0.0 63.2 jit_solution(14214954866090645267)
XLA Ops:
  0.6 58.9 %vocab_xent.1 = (f32[4096,512]{1,0:T(8,128)S(1)}, f32[8,128]{1,0:T(8,128)S(1)}, bf16[256,512]{1,0:T(8,128)(2,1)S(1)}, f32[4,128]{1,0:T(4,128)S(1)}, f32[4,128]{1,0:T(4,128)S(1)}) custom-call(bf16[256,512]{1,0:T(8,128)(2,1)} %hid_hbm.1, f32[1,512]{1,0:T(1,128)} %bitcast.10, f32[1,512]{1,0:T(1,128)} %bitcast.11, bf16[4096,512]{1,0:T(8,128)(2,1)} %e_hbm.1, ...), custom_call_target="tpu_custom_call" | custom-call | tf_op jit(solution)/shard_map/vocab_xent/pallas_call | solution.py:503
  59.5 3.5 %write_out.1 = (f32[2,128]{1,0:T(2,128)}, f32[1,1]{1,0:T(1,128)}, bf16[256,512]{1,0:T(8,128)(2,1)}, f32[4096,512]{1,0:T(8,128)}, f32[4,128]{1,0:T(4,128)}, /*index=5*/f32[4,128]{1,0:T(4,128)}) custom-call(f32[4096,512]{1,0:T(8,128)S(1)} %get-tuple-element.17.de, f32[8,128]{1,0:T(8,128)S(1)} %get-tuple-element.18.loss_in, ...), custom_call_target="tpu_custom_call" | custom-call | tf_op jit(solution)/shard_map/write_out/pallas_call | solution.py:567

commit v6 on v5

--- a/solution.py
+++ b/solution.py
@@ -144,10 +144,11 @@
 
     inputs[5].wait()
 
-    @pl.loop(0, vocab // 128)
+    @pl.loop(0, vocab // 2048)
     def _(i):
-        row = jnp.broadcast_to(valid[pl.ds(i, 1), :].astype(jnp.float32), (128, 128))
-        vb[pl.ds(pl.multiple_of(i * 128, 128), 128), :] = row.T
+        for u in range(16):
+            row = jnp.broadcast_to(valid[pl.ds(i * 16 + u, 1), :].astype(jnp.float32), (128, 128))
+            vb[pl.ds(pl.multiple_of(i * 2048 + u * 128, 128), 128), :] = row.T
 
     for cp in e_copies:
         cp.wait()
@@ -383,9 +384,10 @@
         remote(ref0, ref0, tm_s.at[n], tm_r.at[n], partner).wait_recv()
     ag_pass(0)
 
-    @pl.loop(0, nv)
+    @pl.loop(0, nv // 4)
     def _(i):
-        et[i] = e[pl.ds(pl.multiple_of(i * vc, vc), vc), :].T
+        for u in range(4):
+            et[i * 4 + u] = e[pl.ds(pl.multiple_of((i * 4 + u) * vc, vc), vc), :].T
 
     ag_arrival(0, REL_RIGHT)
     forward((0, RIGHT, 2))

time: 63.2 us -> 61 us (0.965)
  Pallas kernels: 62.3 us -> 60.1 us
    pallas_call x1, Pallas kernels: 58.9 us -> 56.6 us  [group_step(): pl.pallas_call(functools.partial(kernel, vc=vc, ec=ec, n1=n1, n2=n2), out...]
where the time goes in v6:
time: 61 us; the launch traced here: 60.9 us
  Pallas kernels  60.1 us (99%)
  between operations  0.8 us (1%)
    pallas_call x1, Pallas kernels, group_step(): pl.pallas_call(functools.partial(kernel, vc=vc, ec=ec, n1=n1, n2=n2), out...  56.6 us
    pallas_call x1, Pallas kernels, group_step(): pl.pallas_call(functools.partial(write_out, pieces=8), out_shape=(jax.Sha...  3.47 us

profile of v6, /device:TPU:113, one launch (start us, length us, event | category | flops | bytes accessed | tf_op | source)
XLA Modules:
  0.0 60.9 jit_solution(17774234328016338342)
XLA Ops:
  0.6 56.6 %vocab_xent.1 = (f32[4096,512]{1,0:T(8,128)S(1)}, f32[8,128]{1,0:T(8,128)S(1)}, bf16[256,512]{1,0:T(8,128)(2,1)S(1)}, f32[4,128]{1,0:T(4,128)S(1)}, f32[4,128]{1,0:T(4,128)S(1)}) custom-call(bf16[256,512]{1,0:T(8,128)(2,1)} %hid_hbm.1, f32[1,512]{1,0:T(1,128)} %bitcast.10, f32[1,512]{1,0:T(1,128)} %bitcast.11, bf16[4096,512]{1,0:T(8,128)(2,1)} %e_hbm.1, ...), custom_call_target="tpu_custom_call" | custom-call | tf_op jit(solution)/shard_map/vocab_xent/pallas_call | solution.py:505
  57.3 3.5 %write_out.1 = (f32[2,128]{1,0:T(2,128)}, f32[1,1]{1,0:T(1,128)}, bf16[256,512]{1,0:T(8,128)(2,1)}, f32[4096,512]{1,0:T(8,128)}, f32[4,128]{1,0:T(4,128)}, /*index=5*/f32[4,128]{1,0:T(4,128)}) custom-call(f32[4096,512]{1,0:T(8,128)S(1)} %get-tuple-element.17.de, f32[8,128]{1,0:T(8,128)S(1)} %get-tuple-element.18.loss_in, ...), custom_call_target="tpu_custom_call" | custom-call | tf_op jit(solution)/shard_map/write_out/pallas_call | solution.py:569

commit v7 on v6

--- a/solution.py
+++ b/solution.py
@@ -74,11 +74,12 @@
     for cp in inputs[:5]:
         cp.wait()
 
-    for h in range(2):
+    def normalize(h):
         xh, _ = norm(hid[h * HT : (h + 1) * HT, :].astype(jnp.float32))
         x_all[h, c, k] = (xh * gain[...] + bias[...]).astype(jnp.bfloat16)
+
     tm_all[me] = tgt[...] * 2 + msk[...]
-
+    normalize(0)
     pl.semaphore_wait(barrier, group - 1)
 
     def ag(h, i, src, dst, dev):
@@ -131,16 +132,13 @@
     def tm_copy(j):
         return remote(tm_all.at[me], tm_all.at[me], tm_s.at[j - 1], tm_r.at[j - 1], (me + j) % group)
 
-    for h in range(2):
-        if h == 0:
-            for j in range(1, group):
-                go(tm_copy, j)
-        for i in (TO_PARTNER, TO_RIGHT, TO_LEFT):
-            go(ag_copy, h, i)
-
-    def tm_arrival(j):
-        ref = tm_all.at[(me - j + group) % group]
-        remote(ref, ref, tm_s.at[j - 1], tm_r.at[j - 1], partner).wait_recv()
+    for i in (TO_PARTNER, TO_RIGHT, TO_LEFT):
+        go(ag_copy, 0, i)
+    for j in range(1, group):
+        go(tm_copy, j)
+    normalize(1)
+    for i in (TO_PARTNER, TO_RIGHT, TO_LEFT):
+        go(ag_copy, 1, i)
 
     inputs[5].wait()
 

time: 61 us -> 61.1 us (level)
  no operation moved by 1% of the time
where the time goes in v7:
time: 61.1 us; the launch traced here: 61 us
  Pallas kernels  60.2 us (99%)
  between operations  0.8 us (1%)
    pallas_call x1, Pallas kernels, group_step(): pl.pallas_call(functools.partial(kernel, vc=vc, ec=ec, n1=n1, n2=n2), out...  56.7 us
    pallas_call x1, Pallas kernels, group_step(): pl.pallas_call(functools.partial(write_out, pieces=8), out_shape=(jax.Sha...  3.47 us

profile of v7, /device:TPU:113, one launch (start us, length us, event | category | flops | bytes accessed | tf_op | source)
XLA Modules:
  0.0 61.0 jit_solution(6999445968275096528)
XLA Ops:
  0.6 56.7 %vocab_xent.1 = (f32[4096,512]{1,0:T(8,128)S(1)}, f32[8,128]{1,0:T(8,128)S(1)}, bf16[256,512]{1,0:T(8,128)(2,1)S(1)}, f32[4,128]{1,0:T(4,128)S(1)}, f32[4,128]{1,0:T(4,128)S(1)}) custom-call(bf16[256,512]{1,0:T(8,128)(2,1)} %hid_hbm.1, f32[1,512]{1,0:T(1,128)} %bitcast.10, f32[1,512]{1,0:T(1,128)} %bitcast.11, bf16[4096,512]{1,0:T(8,128)(2,1)} %e_hbm.1, ...), custom_call_target="tpu_custom_call" | custom-call | tf_op jit(solution)/shard_map/vocab_xent/pallas_call | solution.py:503
  57.4 3.5 %write_out.1 = (f32[2,128]{1,0:T(2,128)}, f32[1,1]{1,0:T(1,128)}, bf16[256,512]{1,0:T(8,128)(2,1)}, f32[4096,512]{1,0:T(8,128)}, f32[4,128]{1,0:T(4,128)}, /*index=5*/f32[4,128]{1,0:T(4,128)}) custom-call(f32[4096,512]{1,0:T(8,128)S(1)} %get-tuple-element.17.de, f32[8,128]{1,0:T(8,128)S(1)} %get-tuple-element.18.loss_in, ...), custom_call_target="tpu_custom_call" | custom-call | tf_op jit(solution)/shard_map/write_out/pallas_call | solution.py:567
